TPU v7x, 32 devices: a whole 2x2x4 slice. The times are simulated.
32 devices in a mesh: dp: 2 (over x), tp: 16 (over z, y, core).
Axes of the slice: x: 2, y: 2, z: 4, core: 2. Of those that a mesh axis runs over, the one named last changes fastest.
Arguments:
- hidden: bfloat16 [4, 2048, 2048], P('dp'), parts along dimension 0
- lengths: int32 [4], P('dp'), parts along dimension 0
- w_query: bfloat16 [2, 2048, 16, 128], P(None, None, 'tp')
- w_key: bfloat16 [2, 2048, 16, 128], P(None, None, 'tp')
- w_value: bfloat16 [2, 2048, 16, 128], P(None, None, 'tp')
- w_out: bfloat16 [2, 16, 128, 2048], P(None, 'tp')
- w_gate: bfloat16 [2, 2048, 8192], P(None, None, 'tp')
- w_up: bfloat16 [2, 2048, 8192], P(None, None, 'tp')
- w_down: bfloat16 [2, 8192, 2048], P(None, 'tp')
- norm_attn: float32 [2, 2048], replicated
- norm_mlp: float32 [2, 2048], replicated
Outputs:
- output 1: bfloat16 [4, 2048, 2048], P('dp'), parts along dimension 0
- output 2: bfloat16 [2, 4, 16, 2048, 128], P(None, 'dp', 'tp'), parts along dimension 1
- output 3: bfloat16 [2, 4, 16, 2048, 128], P(None, 'dp', 'tp'), parts along dimension 1
There are 2 independent parts. A program takes and returns all parts, laid end to end along the dimension named above; an argument that names none is the same for every part.
All inputs are finite; a program needn't handle non-finite values.
Results may differ from a plain program's by a relative error of at most 0.018908.
Values are sent between devices in bfloat16 or wider.
A program may use at most 1 GiB of HBM per device.

v0:
```python
import jax
import jax.numpy as jnp
from jax import lax
from jax.sharding import PartitionSpec as P

RMS_EPS = 1e-6
ROPE_BASE = 10000.0


def rms_norm(x_in, norm_gain):
    x_f32 = x_in.astype(jnp.float32)
    mean_sq = jnp.mean(x_f32 * x_f32, axis=-1, keepdims=True)
    return (x_f32 * lax.rsqrt(mean_sq + RMS_EPS) * (1.0 + norm_gain)).astype(jnp.bfloat16)


def rope_tables(seq_len, head_dim):
    half_dim = head_dim // 2
    inv_freq = ROPE_BASE ** (-jnp.arange(half_dim, dtype=jnp.float32) * (2.0 / head_dim))
    angles = jnp.arange(seq_len, dtype=jnp.float32)[:, None] * inv_freq[None, :]
    return jnp.cos(angles)[:, None, :], jnp.sin(angles)[:, None, :]


def apply_rope(x_in, cos_t, sin_t):
    half_dim = x_in.shape[-1] // 2
    x_low = x_in[..., :half_dim]
    x_high = x_in[..., half_dim:]
    return jnp.concatenate([x_low * cos_t - x_high * sin_t, x_high * cos_t + x_low * sin_t], axis=-1)


def attention(normed, lengths, w_query, w_key, w_value, cos_t, sin_t):
    head_dim = w_query.shape[-1]
    seq_len = normed.shape[1]
    query = jnp.einsum("duo,ojf->dujf", normed, w_query, preferred_element_type=jnp.float32)
    keys = jnp.einsum("duo,ojf->dujf", normed, w_key, preferred_element_type=jnp.float32)
    values = jnp.einsum("duo,ojf->dujf", normed, w_value, preferred_element_type=jnp.float32).astype(jnp.bfloat16)
    query_rot = (apply_rope(query, cos_t, sin_t) * (head_dim ** -0.5)).astype(jnp.bfloat16)
    key_rot = apply_rope(keys, cos_t, sin_t).astype(jnp.bfloat16)
    scores = jnp.einsum("bqhd,bkhd->bhqk", query_rot, key_rot, preferred_element_type=jnp.float32)
    positions = jnp.arange(seq_len)
    allowed = (positions[None, None, :] <= positions[None, :, None]) & (positions[None, None, :] < lengths[:, None, None])
    scores = jnp.where(allowed[:, None, :, :], scores, -1e30)
    attn_probs = jax.nn.softmax(scores, axis=-1).astype(jnp.bfloat16)
    attn_out = jnp.einsum("bhqk,bkhd->bqhd", attn_probs, values, preferred_element_type=jnp.float32).astype(jnp.bfloat16)
    return attn_out, key_rot, values


def mlp_partial(normed, w_gate, w_up, w_down):
    gate_pre = jnp.einsum("bsm,mf->bsf", normed, w_gate, preferred_element_type=jnp.float32)
    up_proj = jnp.einsum("bsm,mf->bsf", normed, w_up, preferred_element_type=jnp.float32)
    hidden_act = (jax.nn.gelu(gate_pre, approximate=True) * up_proj).astype(jnp.bfloat16)
    return jnp.einsum("bsf,fm->bsm", hidden_act, w_down, preferred_element_type=jnp.float32)


def solution(mesh):
    head_cols = P(None, None, "tp", None)
    head_rows = P(None, "tp", None, None)
    ff_cols = P(None, None, "tp")
    ff_rows = P(None, "tp", None)

    def shard_body(hidden, lengths, w_query, w_key, w_value, w_out, w_gate, w_up, w_down, norm_attn, norm_mlp):
        cos_t, sin_t = rope_tables(hidden.shape[1], w_query.shape[-1])
        hidden_state = hidden
        key_list = []
        value_list = []
        for layer_idx in range(w_query.shape[0]):
            normed = rms_norm(hidden_state, norm_attn[layer_idx])
            attn_out, key_rot, values = attention(normed, lengths, w_query[layer_idx], w_key[layer_idx], w_value[layer_idx], cos_t, sin_t)
            part_sum = jnp.einsum("bqhd,hdm->bqm", attn_out, w_out[layer_idx], preferred_element_type=jnp.float32).astype(jnp.bfloat16)
            summed = lax.psum(part_sum, "tp")
            hidden_state = (hidden_state.astype(jnp.float32) + summed.astype(jnp.float32)).astype(jnp.bfloat16)
            normed = rms_norm(hidden_state, norm_mlp[layer_idx])
            part_sum = mlp_partial(normed, w_gate[layer_idx], w_up[layer_idx], w_down[layer_idx]).astype(jnp.bfloat16)
            summed = lax.psum(part_sum, "tp")
            hidden_state = (hidden_state.astype(jnp.float32) + summed.astype(jnp.float32)).astype(jnp.bfloat16)
            key_list.append(jnp.swapaxes(key_rot, 1, 2))
            value_list.append(jnp.swapaxes(values, 1, 2))
        return hidden_state, jnp.stack(key_list), jnp.stack(value_list)

    return jax.shard_map(
        shard_body,
        mesh=mesh,
        in_specs=(P("dp"), P("dp"), head_cols, head_cols, head_cols, head_rows, ff_cols, ff_cols, ff_rows, P(), P()),
        out_specs=(P("dp"), P(None, "dp", "tp"), P(None, "dp", "tp")),
        check_vma=False,
    )
```

profile of v0, /device:TPU:0, one launch (start us, length us, event | category | flops | bytes accessed | tf_op | source)
XLA Modules:
  0.0 1508.4 jit_solution(14549965392679284141)
XLA Ops:
  13.6 7.2 fusion.2
  20.8 7.7 fusion.74
  28.5 7.7 fusion.77
  38.3 6.7 fusion.86
  46.7 19.6 %fusion.167 = (f32[2,2048]{1,0:T(2,128)S(1)}, f32[2,2048,2048]{1,2,0:T(8,128)}) fusion(pred[2,2048]{1,0:T(4,128)(4,1)S(1)} %iota_compare_fusion.1, pred[2048,2048]{0,1:T(8,128)(4,1)} %iota_compare_fusion, bf16[2,2048,64]{1,2,0:T(8,128)(2,1)S(1)} %bitcast.120, bf16[2,2048,64]{1,2,0:T(8,128)(2,1)S(1)} %bitcast.122, f32[2,2048,64]{1,2,0:T(8,128)} %get-tuple-element.17, ...), kind=kOutput, calls=%fused_computation.166 | convolution fusion | flops 2184710144 | bytes 40914944 | tf_op jit(solution)/shard_map/sub | solution.py:42
  66.4 18.4 %convolution_convert_fusion.3 = bf16[2,2048,2048]{2,1,0:T(8,128)(2,1)} fusion(bf16[2,2048,128]{2,1,0:T(8,128)(2,1)S(1)} %fusion.86, f32[2,2048,2048]{1,2,0:T(8,128)} %get-tuple-element.31, f32[2,2048]{1,0:T(2,128)S(1)} %get-tuple-element.30, bf16[2,1,128,2048]{3,2,1,0:T(8,128)(2,1)} %param.16), kind=kOutput, calls=%fused_computation.56 | convolution fusion | flops 4320657408 | bytes 51920896 | tf_op jit(solution)/shard_map/bqhd,hdm->bqm/dot_general | solution.py:68
  86.1 299.6 %all-reduce.5.cloned.1.call-done = bf16[2,2048,2048]{2,1,0:T(8,128)(2,1)} async-done(((bf16[2,2048,2048]{2,1,0:T(8,128)(2,1)}), bf16[2,2048,2048]{2,1,0:T(8,128)(2,1)}) %all-reduce.5.cloned.1.call-update) | async-done | bytes 16777232 | tf_op jit(solution)/shard_map/psum | solution.py:69
  385.7 14.7 fusion.6
  406.6 13.0 fusion.32
  419.6 16.9 %fusion.56 = bf16[2,2048,512]{2,1,0:T(8,128)(2,1)S(1)} fusion(f32[2,2048,512]{2,1,0:T(8,128)} %fusion.32, bf16[2,2048,2048]{2,1,0:T(8,128)(2,1)} %copy-done.3, f32[2048]{0:T(1024)S(1)} %bitcast.136, f32[2,2048]{1,0:T(2,128)S(1)} %add_rsqrt_fusion.2, bf16[2,2048,512]{2,1,0:T(8,128)(2,1)} %param.17), kind=kOutput, calls=%fused_computation.71 | convolution fusion | flops 8644460544 | bytes 31481856 | tf_op jit(solution)/shard_map/bsm,mf->bsf/dot_general | solution.py:48
  436.6 11.9 convolution_convert_fusion.1
  448.6 297.7 %all-reduce.7.cloned.1.call-done = bf16[2,2048,2048]{2,1,0:T(8,128)(2,1)} async-done(((bf16[2,2048,2048]{2,1,0:T(8,128)(2,1)}), bf16[2,2048,2048]{2,1,0:T(8,128)(2,1)}) %all-reduce.7.cloned.1.call-update) | async-done | bytes 16777232 | tf_op jit(solution)/shard_map/psum | solution.py:73
  746.3 14.7 fusion.10
  761.1 8.1 fusion.83
  769.1 7.7 fusion.80
  785.1 19.6 %fusion.172 = (f32[2,2048]{1,0:T(2,128)S(1)}, f32[2,2048,2048]{1,2,0:T(8,128)}) fusion(pred[2,2048]{1,0:T(4,128)(4,1)S(1)} %copy-done.24, pred[2048,2048]{0,1:T(8,128)(4,1)} %iota_compare_fusion, bf16[2,2048,64]{1,2,0:T(8,128)(2,1)S(1)} %bitcast.124, bf16[2,2048,64]{1,2,0:T(8,128)(2,1)S(1)} %bitcast.126, f32[2,2048,64]{1,2,0:T(8,128)} %get-tuple-element.13, ...), kind=kOutput, calls=%fused_computation.167 | convolution fusion | flops 2184710144 | bytes 40914944 | tf_op jit(solution)/shard_map/sub | solution.py:42
  804.8 18.4 %convolution_convert_fusion.2 = bf16[2,2048,2048]{2,1,0:T(8,128)(2,1)} fusion(bf16[2,2048,128]{2,1,0:T(8,128)(2,1)S(1)} %fusion.89, f32[2,2048,2048]{1,2,0:T(8,128)} %get-tuple-element.33, f32[2,2048]{1,0:T(2,128)S(1)} %get-tuple-element.32, bf16[2,1,128,2048]{3,2,1,0:T(8,128)(2,1)} %param.16), kind=kOutput, calls=%fused_computation.55 | convolution fusion | flops 4320657408 | bytes 51920896 | tf_op jit(solution)/shard_map/bqhd,hdm->bqm/dot_general | solution.py:68
  823.2 297.7 %all-reduce.9.cloned.1.call-done = bf16[2,2048,2048]{2,1,0:T(8,128)(2,1)} async-done(((bf16[2,2048,2048]{2,1,0:T(8,128)(2,1)}), bf16[2,2048,2048]{2,1,0:T(8,128)(2,1)}) %all-reduce.9.cloned.1.call-update) | async-done | bytes 16777232 | tf_op jit(solution)/shard_map/psum | solution.py:69
  1120.9 14.7 fusion.14
  1141.8 13.1 fusion.28
  1154.9 17.0 %fusion.65 = bf16[2,2048,512]{2,1,0:T(8,128)(2,1)S(1)} fusion(f32[2,2048,512]{2,1,0:T(8,128)} %fusion.28, bf16[2,2048,2048]{2,1,0:T(8,128)(2,1)} %copy-done, f32[2048]{0:T(1024)S(1)} %bitcast.131, f32[2,2048]{1,0:T(2,128)S(1)} %add_rsqrt_fusion, bf16[2,2048,512]{2,1,0:T(8,128)(2,1)} %param.17), kind=kOutput, calls=%fused_computation.80 | convolution fusion | flops 8644460544 | bytes 31481856 | tf_op jit(solution)/shard_map/bsm,mf->bsf/dot_general | solution.py:48
  1171.8 12.0 convolution_convert_fusion
  1191.9 289.7 %all-reduce.11.cloned.1.call-done = bf16[2,2048,2048]{2,1,0:T(8,128)(2,1)} async-done(((bf16[2,2048,2048]{2,1,0:T(8,128)(2,1)}), bf16[2,2048,2048]{2,1,0:T(8,128)(2,1)}) %all-reduce.11.cloned.1.call-update) | async-done | bytes 16777232 | tf_op jit(solution)/shard_map/psum | solution.py:73
  1481.6 19.8 %fusion.17 = bf16[2,2048,2048]{2,1,0:T(8,128)(2,1)} fusion(bf16[2,2048,2048]{2,1,0:T(8,128)(2,1)} %copy-done, bf16[2,2048,2048]{2,1,0:T(8,128)(2,1)} %all-reduce.11.cloned.1.call-done), kind=kLoop, calls=%fused_computation.31 | loop fusion | flops 33554432 | bytes 50331648 | tf_op jit(solution)/shard_map/convert_element_type | solution.py:74
  (86 shorter events, 40.3 us)
Async XLA Ops:
  7.2 378.5 %all-reduce.5.cloned.1.call-start = ((), (), s32[]{:S(2)}) async-start(), calls=%async_computation | async-start | bytes 33554432 | tf_op jit(solution)/shard_map/psum | solution.py:69
  7.2 13.6 copy-start.1
  13.6 14.9 copy-start.27
  20.8 15.4 %copy-start.21 = (f32[2,2048]{1,0:T(2,128)}, f32[2,2048]{1,0:T(2,128)S(1)}, u32[]{:S(2)}) copy-start(f32[2,2048]{1,0:T(2,128)S(1)} %add_rsqrt_fusion.3) | copy-start | bytes 49156
  28.5 9.6 copy-start.28
  38.1 6.9 copy-start.4
  38.1 6.9 copy-start.6
  38.2 8.5 copy-start.23
  45.0 21.4 %copy-start.18 = (bf16[2,2048,128]{2,1,0:T(8,128)(2,1)}, bf16[2,2048,128]{2,1,0:T(8,128)(2,1)S(1)}, u32[]{:S(2)}) copy-start(bf16[2,2048,128]{2,1,0:T(8,128)(2,1)S(1)} %fusion.86) | copy-start | bytes 3145732
  46.7 19.6 %copy-start.12 = (bf16[2,2048,1,64]{1,3,0,2:T(8,128)(2,1)}, bf16[2,2048,1,64]{1,3,0,2:T(8,128)(2,1)S(1)}, u32[]{:S(2)}) copy-start(bf16[2,2048,1,64]{1,3,0,2:T(8,128)(2,1)S(1)} %get-tuple-element.22) | copy-start | bytes 1572868
  46.7 19.6 %copy-start.14 = (bf16[2,2048,1,64]{1,3,0,2:T(8,128)(2,1)}, bf16[2,2048,1,64]{1,3,0,2:T(8,128)(2,1)S(1)}, u32[]{:S(2)}) copy-start(bf16[2,2048,1,64]{1,3,0,2:T(8,128)(2,1)S(1)} %get-tuple-element.23) | copy-start | bytes 1572868
  84.8 661.5 %all-reduce.7.cloned.1.call-start = ((), (), s32[]{:S(2)}) async-start(), calls=%async_computation.1 | async-start | bytes 33554432 | tf_op jit(solution)/shard_map/psum | solution.py:73
  419.6 17.0 %copy-start.29 = (bf16[2,512,2048]{2,1,0:T(8,128)(2,1)S(1)}, bf16[2,512,2048]{2,1,0:T(8,128)(2,1)}, u32[]{:S(2)}) copy-start(bf16[2,512,2048]{2,1,0:T(8,128)(2,1)} %param.19) | copy-start | bytes 12582916
  448.5 312.5 %copy-start.26 = (f32[1,2048]{1,0:T(1,128)S(1)}, f32[1,2048]{1,0:T(1,128)}, u32[]{:S(2)}) copy-start(f32[1,2048]{1,0:T(1,128)} %get-tuple-element.26) | copy-start | bytes 24580
  448.5 672.4 %all-reduce.9.cloned.1.call-start = ((), (), s32[]{:S(2)}) async-start(), calls=%async_computation.2 | async-start | bytes 33554432 | tf_op jit(solution)/shard_map/psum | solution.py:69
  761.0 15.8 %copy-start.2 = (bf16[2,2048,2048]{2,1,0:T(8,128)(2,1)}, bf16[2,2048,2048]{2,1,0:T(8,128)(2,1)S(1)}, u32[]{:S(2)}) copy-start(bf16[2,2048,2048]{2,1,0:T(8,128)(2,1)S(1)} %get-tuple-element.9) | copy-start | bytes 50331652
  761.0 8.1 copy-start.22
  776.8 8.3 copy-start.24
  783.4 21.3 %copy-start.19 = (bf16[2,2048,128]{2,1,0:T(8,128)(2,1)}, bf16[2,2048,128]{2,1,0:T(8,128)(2,1)S(1)}, u32[]{:S(2)}) copy-start(bf16[2,2048,128]{2,1,0:T(8,128)(2,1)S(1)} %fusion.89) | copy-start | bytes 3145732
  785.1 19.6 %copy-start.16 = (bf16[2,2048,1,64]{1,3,0,2:T(8,128)(2,1)}, bf16[2,2048,1,64]{1,3,0,2:T(8,128)(2,1)S(1)}, u32[]{:S(2)}) copy-start(bf16[2,2048,1,64]{1,3,0,2:T(8,128)(2,1)S(1)} %get-tuple-element.20) | copy-start | bytes 1572868
  785.1 19.6 %copy-start.17 = (bf16[2,2048,1,64]{1,3,0,2:T(8,128)(2,1)}, bf16[2,2048,1,64]{1,3,0,2:T(8,128)(2,1)S(1)}, u32[]{:S(2)}) copy-start(bf16[2,2048,1,64]{1,3,0,2:T(8,128)(2,1)S(1)} %get-tuple-element.21) | copy-start | bytes 1572868
  823.1 318.7 %copy-start.25 = (f32[1,2048]{1,0:T(1,128)S(1)}, f32[1,2048]{1,0:T(1,128)}, u32[]{:S(2)}) copy-start(f32[1,2048]{1,0:T(1,128)} %get-tuple-element.24) | copy-start | bytes 24580
  823.1 658.5 %all-reduce.11.cloned.1.call-start = ((), (), s32[]{:S(2)}) async-start(), calls=%async_computation.3 | async-start | bytes 33554432 | tf_op jit(solution)/shard_map/psum | solution.py:73
  1154.9 17.0 %copy-start.30 = (bf16[2,512,2048]{2,1,0:T(8,128)(2,1)S(1)}, bf16[2,512,2048]{2,1,0:T(8,128)(2,1)}, u32[]{:S(2)}) copy-start(bf16[2,512,2048]{2,1,0:T(8,128)(2,1)} %param.19) | copy-start | bytes 12582916
  (11 other events, 55.2 us)
Sparse Core Ops, SparseCore 0:
  84.9 300.7 all-reduce.4
  448.6 297.6 all-reduce.6
  823.3 297.6 all-reduce.8
  1183.9 297.6 all-reduce.10
where the time goes:
time: 1520 us; the launch traced here: 1510 us
  waiting for transfers between devices  1180 us (78%)
  matrix products  204 us (13%)
  other arithmetic  88 us (6%)
  local copies, waits for them, and re-layouts  16.7 us (1%)
    psum x4, waiting for transfers between devices, shard_body(): summed = lax.psum(part_sum, 'tp')  1180 us
    reduce_sum x4, other arithmetic, rms_norm(): mean_sq = jnp.mean(x_f32 * x_f32, axis=-1, keepdims=True)  51.3 us
    sub x2, matrix products, attention(): attn_probs = jax.nn.softmax(scores, axis=-1).astype(jnp.bfloat16)  39.2 us
    dot_general x2, matrix products, shard_body(): jnp.einsum('bqhd,hdm->bqm', attn_out, w_out[layer_idx], preferred_element...  36.7 us
    dot_general x2, matrix products, mlp_partial(): jnp.einsum('bsm,mf->bsf', normed, w_gate, preferred_element_type=jnp.floa...  33.9 us
  transfers between devices with their start and end apart: 4, of which 4 were waited for; matrix products, arithmetic and copies ran while one was open for 0% of the time, Pallas kernels for 0%

commit v1 on v0

v1 whole, which is shorter than its diff:
```python
import functools

import jax
import jax.numpy as jnp
import numpy as np
from jax import lax
from jax.experimental import pallas as pl
from jax.experimental.pallas import tpu as pltpu
from jax.sharding import PartitionSpec as P

RMS_EPS = 1e-6
ROPE_BASE = 10000.0
CHUNK = 128
RING = 8
F32 = jnp.float32
BF16 = jnp.bfloat16
MESH = pl.DeviceIdType.MESH


def rope_table(seq_len, head_dim):
    half = head_dim // 2
    inv_freq = np.float32(ROPE_BASE) ** (-np.arange(half, dtype=np.float32) * np.float32(2.0 / head_dim))
    angles = np.arange(seq_len, dtype=np.float32)[:, None] * inv_freq[None, :].astype(np.float32)
    angles = angles.astype(np.float64)
    return np.concatenate([np.cos(angles), np.sin(angles)], axis=-1).astype(np.float32)


def layers_kernel(C, hid, lens, wq, wk, wv, wo, wg, wu, wd, ga, gm, rope,
                  h, kc, vc, lq, lk, lv, lo, lg, lu, ld,
                  x, xo, a, wqkv, wov, wgv, wuv, wdv, ropev, kb, vb, sc, ob, osend, mb, pb, d2d, ts, ro, ri,
                  s_ch, s_yh, s_one, s_kv, s_o, s_x, s_xo, s_wl, s_ys, s_xs, s_xr, s_yr):
    S, D = x.shape
    HD = wq.shape[2]
    FL = wg.shape[2]
    n = S // C
    H2, H4 = C // 2, C // 4
    NB = RING
    KB = sc.shape[2]
    RB = 16

    dp = lax.axis_index("dp")
    tp = lax.axis_index("tp")
    c = lax.rem(tp, 2)
    y = lax.rem(tp // 2, 2)
    z = tp // 4
    left = z < 2
    inner = (z == 1) | (z == 2)
    outer = (z == 0) | (z == 3)
    step = jnp.where(left, 4, -4)
    sib = (dp, tp + 1 - 2 * c)
    ypart = (dp, tp + 2 - 4 * y)
    xpart = (1 - dp, tp)
    inward = (dp, tp + step)
    outward = (dp, jnp.where(inner, tp - step, tp))
    off_a = pl.multiple_of(jnp.where(left, 0, H4), H4)
    off_b = pl.multiple_of(jnp.where(left, H4, 0), H4)
    my = pl.multiple_of(c * H2, H2)
    his = pl.multiple_of((1 - c) * H2, H2)

    barrier = pltpu.get_barrier_semaphore()
    for dev in (sib, ypart, xpart, inward):
        pl.semaphore_signal(barrier, inc=1, device_id=dev, device_id_type=MESH)

    @pl.when(inner)
    def _():
        pl.semaphore_signal(barrier, inc=1, device_id=outward, device_id_type=MESH)

    pl.semaphore_wait(barrier, jnp.where(inner, 5, 4))

    def rcopy(src, dst, ss, rs, dev):
        return pltpu.make_async_remote_copy(src_ref=src, dst_ref=dst, send_sem=ss, recv_sem=rs, device_id=dev, device_id_type=MESH)

    lcopy = pltpu.make_async_copy

    tensors = [(wo, 0, lo.at[0], HD, 1), (wg, 0, lg.at[0], D, 4), (wu, 0, lu.at[0], D, 4), (wd, 0, ld.at[0], FL, 4),
               (wq, 1, lq, D, 1), (wk, 1, lk, D, 1), (wv, 1, lv, D, 1), (wo, 1, lo.at[1], HD, 1),
               (wg, 1, lg.at[1], D, 4), (wu, 1, lu.at[1], D, 4), (wd, 1, ld.at[1], FL, 4)]
    first = [0]
    for t in tensors:
        first.append(first[-1] + t[4])
    pieces = first[-1]
    rate = 16 // n if n < 16 else 1
    lead = 3

    def part_rows(t, part):
        half = tensors[t][3] // 2
        size = half // tensors[t][4]
        return pl.ds(pl.multiple_of(dp * half + part * size, size), size)

    def over_y(t, part):
        src, layer, land, _, _ = tensors[t]
        rows = part_rows(t, part)
        return rcopy(src.at[layer, rows], land.at[rows], s_ys.at[t], s_yr.at[first[t] + part], ypart)

    def over_x(t, part):
        land = tensors[t][2]
        rows = part_rows(t, part)
        return rcopy(land.at[rows], land.at[rows], s_xs.at[t], s_xr.at[t], xpart)

    def half_of(t):
        src, layer, land, full, _ = tensors[t]
        return land.at[pl.ds(0, full // 2)]

    def wait_xr(t):
        rcopy(half_of(t), half_of(t), s_xs.at[t], s_xr.at[t], xpart).wait_recv()

    def wait_sends(t):
        rcopy(half_of(t), half_of(t), s_ys.at[t], s_yr.at[first[t]], ypart).wait_send()
        rcopy(half_of(t), half_of(t), s_xs.at[t], s_xr.at[t], xpart).wait_send()

    def load(i, layer):
        j, kind = divmod(i, 7)
        if j == 0:
            src = (wq, wk, wv, wo, wg, wu, wd)[kind].at[layer]
        else:
            src = (lq, lk, lv, lo.at[layer], lg.at[layer], lu.at[layer], ld.at[layer])[kind]
        dst = (wqkv.at[j, :, pl.ds(0, HD)], wqkv.at[j, :, pl.ds(HD, HD)], wqkv.at[j, :, pl.ds(2 * HD, HD)],
               wov.at[pl.ds(j * HD, HD)], wgv.at[j], wuv.at[j], wdv.at[pl.ds(j * FL, FL)])[kind]
        return lcopy(src, dst, s_wl.at[i])

    def base(k):
        return pl.multiple_of(lax.rem(k, n) * C, C)

    def ch(i, k):
        return s_ch.at[i, lax.rem(k, NB)]

    def h_d2d(k):
        kk = lax.rem(k, NB)
        return rcopy(pb.at[kk, pl.ds(his, H2)], d2d.at[kk], ch(0, k), ch(1, k), sib)

    def h_up(k):
        kk = lax.rem(k, NB)
        return rcopy(ts.at[kk], ro.at[kk], ch(2, k), ch(3, k), inward)

    def h_mid(k):
        kk = lax.rem(k, NB)
        return rcopy(ts.at[kk, pl.ds(0, H4)], ri.at[kk], ch(4, k), ch(5, k), inward)

    def rows_of(k, off, size):
        return x.at[pl.ds(pl.multiple_of(base(k) + my + off, H4), size)]

    def h_fi(k):
        return rcopy(rows_of(k, off_b, H4), rows_of(k, off_b, H4), ch(6, k), ch(7, k), inward)

    def h_fo(k, off, size):
        return rcopy(rows_of(k, off, size), rows_of(k, off, size), ch(8, k), ch(9, k), outward)

    def h_fo_recv(k):
        return rcopy(rows_of(k, 0, H2), rows_of(k, 0, H2), ch(8, k), ch(9, k), inward)

    def h_fs(k):
        return rcopy(rows_of(k, 0, H2), rows_of(k, 0, H2), ch(10, k), ch(11, k), sib)

    def out_rows(k):
        return pl.ds(pl.multiple_of(base(k) + my, H2), H2)

    def h_yh(k):
        return rcopy(rows_of(k, 0, H2), h.at[y, out_rows(k)], s_one.at[0], s_yh.at[lax.rem(k, NB)], ypart)

    def h_yh_recv(k):
        return rcopy(rows_of(k, 0, H2), h.at[1 - y, out_rows(k)], s_one.at[0], s_yh.at[lax.rem(k, NB)], ypart)

    def h_hs(k):
        return rcopy(h.at[1 - y, out_rows(k)], h.at[1 - y, out_rows(k)], s_one.at[1], s_one.at[2], sib)

    def h_local(k):
        rows = pl.ds(base(k), C)
        return lcopy(x.at[rows], h.at[y, rows], s_one.at[3])

    def norm(read, write, gain):
        for r in range(0, C, RB):
            v = read(r).astype(F32)
            ms = jnp.mean(v * v, axis=-1, keepdims=True)
            write(r, (v * lax.rsqrt(ms + RMS_EPS) * gain).astype(BF16))

    def x_chunk(b):
        return lambda r: x[pl.ds(pl.multiple_of(b + r, RB), RB), :]

    def a_write(j):
        def write(r, v):
            a[j, r:r + RB, :] = v
        return write

    def kv_copy(j, which, na, layer, i, remote):
        src = (kb, vb)[which].at[j, pl.ds(pl.multiple_of(i * C, C), C)]
        out = (kc, vc)[which]
        rows = pl.ds(pl.multiple_of(i * C, C), C)
        sem = s_kv.at[lax.rem(na, 2), 2 * j + which]
        if remote:
            return rcopy(src, out.at[1, y, rows], sem, s_one.at[4 + which], ypart)
        b = y if j == 0 else 1 - y
        return lcopy(src, out.at[layer, b, rows], sem)

    def kv_wait(na):
        for which in range(2):
            kv_copy(0, which, na, 0, 0, False).wait()

            @pl.when(na < n)
            def _(which=which):
                kv_copy(1, which, na, 0, 0, False).wait()

            @pl.when(na >= n)
            def _(which=which):
                kv_copy(1, which, na, 0, 0, True).wait_send()

    def o_copy(na):
        par = lax.rem(na, 2)
        return rcopy(osend.at[par], ob.at[par, 1], s_o.at[0, par], s_o.at[1, par], ypart)

    def xo_load(i):
        par = lax.rem(i, 2)
        return lcopy(hid.at[1 - y, pl.ds(pl.multiple_of(i * C, C), C)], xo.at[par], s_xo.at[par])

    def x_load(i):
        rows = pl.ds(pl.multiple_of(i * C, C), C)
        return lcopy(hid.at[y, rows], x.at[rows], s_x.at[i])

    def lanes(op, v):
        out = v[:, 0:128]
        for q in range(128, v.shape[1], 128):
            out = op(out, v[:, q:q + 128])
        return out

    def attn(u):
        stage = u // n
        layer = stage // 2
        i = u - stage * n
        na = layer * n + i
        par = lax.rem(na, 2)
        r0 = pl.multiple_of(i * C, C)

        @pl.when(na >= 2)
        def _():
            kv_wait(na - 2)

        gain = 1.0 + ga[pl.ds(layer, 1), :]

        @pl.when(layer == 0)
        def _():
            x_load(i).wait()
            xo_load(i).wait()

            @pl.when(i + 1 < n)
            def _():
                xo_load(i + 1).start()

            norm(lambda r: xo[par, r:r + RB, :], a_write(1), gain)

        norm(x_chunk(r0), a_write(0), gain)

        tab = ropev[pl.ds(r0, C), :]
        rolled = pltpu.roll(tab, HD // 2, 1)
        low = lax.broadcasted_iota(jnp.int32, (C, HD), 1) < HD // 2
        cos_t = jnp.where(low, tab, rolled)
        sin_t = jnp.where(low, -rolled, tab)

        def rot(v):
            return v * cos_t + pltpu.roll(v, HD // 2, 1) * sin_t

        blocks = (i * C + C + KB - 1) // KB
        for j in (1, 0):
            aj = 0 if j == 0 else 1 - layer
            wj = 0 if j == 0 else layer
            qkv = jnp.dot(a[aj], wqkv[wj], preferred_element_type=F32)
            q = (rot(qkv[:, 0:HD]) * HD ** -0.5).astype(BF16)
            kb[j, pl.ds(r0, C), :] = rot(qkv[:, HD:2 * HD]).astype(BF16)
            vb[j, pl.ds(r0, C), :] = qkv[:, 2 * HD:3 * HD].astype(BF16)
            for which in range(2):
                if j == 0:
                    kv_copy(0, which, na, layer, i, False).start()
                else:
                    @pl.when(layer == 0)
                    def _(which=which):
                        kv_copy(1, which, na, 0, i, False).start()

                    @pl.when(layer == 1)
                    def _(which=which):
                        kv_copy(1, which, na, 1, i, True).start()

            length = lens[y if j == 0 else y * layer + (1 - y) * (1 - layer)]
            limit = jnp.minimum(lax.broadcasted_iota(jnp.int32, (C, KB), 0) + (r0 + 1), length)
            cols = lax.broadcasted_iota(jnp.int32, (C, KB), 1)

            def scores(b, m, j=j, q=q, limit=limit, cols=cols):
                keys = kb[j, pl.ds(pl.multiple_of(b * KB, KB), KB), :]
                s = lax.dot_general(q, keys, (((1,), (1,)), ((), ())), preferred_element_type=F32)
                s = jnp.where(cols + b * KB < limit, s, -1e30)
                sc[b] = s
                return jnp.maximum(m, lanes(jnp.maximum, s))

            m = lax.fori_loop(0, blocks, scores, jnp.full((C, 128), -1e30, F32))
            m = jnp.max(m, axis=1, keepdims=True)

            def exps(b, l, m=m):
                e = jnp.exp(sc[b] - m)
                sc[b] = e
                return l + lanes(jnp.add, e)

            l = lax.fori_loop(0, blocks, exps, jnp.zeros((C, 128), F32))
            inv = 1.0 / jnp.sum(l, axis=1, keepdims=True)

            def mix(b, o, j=j, inv=inv):
                p = (sc[b] * inv).astype(BF16)
                return o + jnp.dot(p, vb[j, pl.ds(pl.multiple_of(b * KB, KB), KB), :], preferred_element_type=F32)

            o = lax.fori_loop(0, blocks, mix, jnp.zeros((C, HD), F32)).astype(BF16)
            if j == 0:
                ob[par, 0] = o
            else:
                @pl.when(layer == 0)
                def _(o=o):
                    @pl.when(i >= 2)
                    def _():
                        o_copy(na - 2).wait_send()

                    osend[par] = o
                    o_copy(na).start()

                @pl.when(layer == 1)
                def _(o=o):
                    ob[par, 1] = o

    NBLK = min(512, D)

    def out_proj(s):
        layer = s // (2 * n)
        par = lax.rem(layer * n + lax.rem(s, n), 2)

        @pl.when(layer == 0)
        def _():
            o_copy(lax.rem(s, n)).wait_recv()

        o = jnp.concatenate([ob[par, 0], ob[par, 1]], axis=1)
        for q in range(0, D, NBLK):
            pb[lax.rem(s, NB), :, q:q + NBLK] = jnp.dot(o, wov[:, q:q + NBLK], preferred_element_type=F32).astype(BF16)

    def mlp(s):
        layer = s // (2 * n)
        norm(x_chunk(base(s)), a_write(0), 1.0 + gm[pl.ds(layer, 1), :])
        FB = min(256, FL)
        for j in range(2):
            for f in range(0, FL, FB):
                g = jnp.dot(a[0], wgv[j, :, f:f + FB], preferred_element_type=F32)
                u = jnp.dot(a[0], wuv[j, :, f:f + FB], preferred_element_type=F32)
                mb[:, j * FL + f:j * FL + f + FB] = (jax.nn.gelu(g, approximate=True) * u).astype(BF16)
        m = mb[...]
        for q in range(0, D, NBLK):
            pb[lax.rem(s, NB), :, q:q + NBLK] = jnp.dot(m, wdv[:, q:q + NBLK], preferred_element_type=F32).astype(BF16)

    def send_up(k):
        h_d2d(k).wait_recv()
        kk = lax.rem(k, NB)
        for r in range(0, H2, RB):
            rr = pl.ds(pl.multiple_of(my + r, RB), RB)
            ts[kk, r:r + RB, :] = (pb[kk, rr, :].astype(F32) + d2d[kk, r:r + RB, :].astype(F32)).astype(BF16)
        h_up(k).start()

    def part(k, off, r):
        kk = lax.rem(k, NB)
        mine = pl.ds(pl.multiple_of(my + off + r, RB), RB)
        rr = pl.ds(pl.multiple_of(off + r, RB), RB)
        return pb[kk, mine, :].astype(F32) + d2d[kk, rr, :].astype(F32) + ro[kk, rr, :].astype(F32)

    def exchange(k):
        h_d2d(k).wait_recv()
        h_up(k).wait_recv()
        kk = lax.rem(k, NB)
        for r in range(0, H4, RB):
            ts[kk, r:r + RB, :] = part(k, off_a, r).astype(BF16)
        h_mid(k).start()

    def finish(k):
        h_mid(k).wait_recv()
        kk = lax.rem(k, NB)
        for r in range(0, H4, RB):
            rows = pl.ds(pl.multiple_of(base(k) + my + off_b + r, RB), RB)
            total = part(k, off_b, r) + ri[kk, r:r + RB, :].astype(F32)
            x[rows, :] = (x[rows, :].astype(F32) + total).astype(BF16)
        h_fi(k).start()
        h_fo(k, off_b, H4).start()

    def last_stage(k):
        return k >= 3 * n

    def pass_on(k):
        h_fi(k).wait_recv()
        h_fo(k, off_a, H4).start()
        h_fs(k).start()

        @pl.when(last_stage(k))
        def _():
            h_yh(k).start()

    def share(k):
        h_fo_recv(k).wait_recv()
        h_fs(k).start()

        @pl.when(last_stage(k))
        def _():
            h_yh(k).start()

    def retire(k):
        h_fs(k).wait_recv()
        h_fs(k).wait_send()
        h_d2d(k).wait_send()

        @pl.when(outer)
        def _():
            h_up(k).wait_send()

        @pl.when(inner)
        def _():
            h_mid(k).wait_send()
            h_fi(k).wait_send()
            h_fo(k, 0, H2).wait_send()

        @pl.when(last_stage(k))
        def _():
            h_local(k).start()

    def forward_out(k):
        h_yh_recv(k).wait_recv()
        h_hs(k).start()

    def at(k, what, cond=None):
        ok = (k >= 0) & (k < 4 * n)
        if cond is not None:
            ok = ok & cond
        pl.when(ok)(lambda: what(k))

    over_y(0, 0).start()
    x_load(0).start()
    xo_load(0).start()
    rope_copy = lcopy(rope, ropev, s_one.at[6])
    rope_copy.start()
    for i in (0, 1, 2, 3):
        load(i, 0).start()
    for p in range(1, lead):
        over_y(1, p - 1).start()
    for i in range(1, n):
        x_load(i).start()
    for i in (4, 5, 6):
        load(i, 0).start()
    for j in range(2):
        for r in range(0, S, KB):
            kb[j, r:r + KB, :] = jnp.zeros((KB, HD), BF16)
            vb[j, r:r + KB, :] = jnp.zeros((KB, HD), BF16)
    rope_copy.wait()
    for i in (0, 1, 2):
        load(i, 0).wait()

    def slot(s, carry):
        at(s - 5, retire)

        @pl.when(s == n)
        def _():
            for i in (4, 5, 6, 11, 12, 13):
                load(i, 0).wait()

        @pl.when(s == 3 * n)
        def _():
            for i in (4, 5, 6, 11, 12, 13):
                load(i, 1).wait()

        @pl.when(s == 2 * n - 1)
        def _():
            for i in (0, 1, 2, 3, 7, 8, 9, 10):
                load(i, 1).wait()

        ok = (s >= 0) & (s < 4 * n)
        is_mlp = lax.rem(s // n, 2) == 1

        @pl.when(ok & is_mlp)
        def _():
            mlp(s)

        @pl.when(ok & jnp.logical_not(is_mlp))
        def _():
            out_proj(s)

        at(s, lambda k: h_d2d(k).start())

        u = s + 1

        @pl.when((u < n) | ((u >= 2 * n) & (u < 3 * n)))
        def _():
            attn(u)

        at(s - 4, share, outer)
        at(s - 3, pass_on, inner)
        at(s - 2, finish, inner)
        at(s - 1, exchange, inner)
        at(s, send_up, outer)
        at(s - 6, forward_out, s - 6 >= 3 * n)

        @pl.when(s == -1)
        def _():
            over_y(0, 0).wait_recv()
            over_x(0, 0).start()
            wait_xr(0)
            load(10, 0).start()
            load(3, 0).wait()
            load(10, 0).wait()

        for r in range(rate):
            for t in range(1, len(tensors)):
                p = s * rate + r + lead - first[t]

                @pl.when((s >= 0) & (p >= 0) & (p < tensors[t][4]))
                def _(t=t, p=p):
                    over_y(t, p).start()

                q = s * rate + r - first[t]

                @pl.when((s >= 0) & (q >= 0) & (q < tensors[t][4]))
                def _(t=t, q=q):
                    over_y(t, q).wait_recv()
                    over_x(t, q).start()

        for t, when, i in ((1, n // 2, 11), (2, 3 * n // 4, 12), (3, n - 1, 13)):
            @pl.when(s == when)
            def _(t=t, i=i):
                wait_xr(t)
                load(i, 0).start()

        @pl.when(s == n + n // 2)
        def _():
            for t in (4, 5, 6, 7):
                wait_xr(t)
            for i in (0, 1, 2, 3, 7, 8, 9, 10):
                load(i, 1).start()

        @pl.when(s == 2 * n)
        def _():
            for t in (8, 9, 10):
                wait_xr(t)
            for i in (4, 5, 6, 11, 12, 13):
                load(i, 1).start()

        return carry

    lax.fori_loop(-1, 4 * n + 6, slot, 0)

    for t in range(len(tensors)):
        wait_sends(t)
    for na in (n - 2, n - 1):
        o_copy(na).wait_send()
    for na in (2 * n - 2, 2 * n - 1):
        kv_wait(na)
    for which, out in ((0, kc), (1, vc)):
        rcopy(out.at[1, 1 - y], out.at[1, 1 - y], s_kv.at[0, 2 + which], s_one.at[4 + which], ypart).wait_recv()
    halfs = h.at[0, pl.ds(0, S // 2)]
    rcopy(halfs, halfs, s_one.at[0], s_yh.at[0], ypart).wait_send()
    rcopy(halfs, halfs, s_one.at[1], s_one.at[2], sib).wait()
    lcopy(x, h.at[y], s_one.at[3]).wait()


def run_layers(hidden, lengths, w_query, w_key, w_value, w_out, w_gate, w_up, w_down, norm_attn, norm_mlp):
    B, S, D = hidden.shape
    L, _, _, HD = w_query.shape
    FL = w_gate.shape[2]
    C = CHUNK
    n = S // C
    KB = min(256, S)
    any_space = pl.BlockSpec(memory_space=pl.ANY)
    vmem = pl.BlockSpec(memory_space=pltpu.VMEM)
    dma = pltpu.SemaphoreType.DMA
    outs = pl.pallas_call(
        functools.partial(layers_kernel, C),
        out_shape=[
            jax.ShapeDtypeStruct((B, S, D), BF16),
            jax.ShapeDtypeStruct((L, B, S, HD), BF16),
            jax.ShapeDtypeStruct((L, B, S, HD), BF16),
            jax.ShapeDtypeStruct((D, HD), BF16),
            jax.ShapeDtypeStruct((D, HD), BF16),
            jax.ShapeDtypeStruct((D, HD), BF16),
            jax.ShapeDtypeStruct((L, HD, D), BF16),
            jax.ShapeDtypeStruct((L, D, FL), BF16),
            jax.ShapeDtypeStruct((L, D, FL), BF16),
            jax.ShapeDtypeStruct((L, FL, D), BF16),
        ],
        in_specs=[any_space, pl.BlockSpec(memory_space=pltpu.SMEM)] + [any_space] * 7 + [vmem, vmem, any_space],
        out_specs=[any_space] * 10,
        scratch_shapes=[
            pltpu.VMEM((S, D), BF16),
            pltpu.VMEM((2, C, D), BF16),
            pltpu.VMEM((2, C, D), BF16),
            pltpu.VMEM((2, D, 3 * HD), BF16),
            pltpu.VMEM((2 * HD, D), BF16),
            pltpu.VMEM((2, D, FL), BF16),
            pltpu.VMEM((2, D, FL), BF16),
            pltpu.VMEM((2 * FL, D), BF16),
            pltpu.VMEM((S, HD), F32),
            pltpu.VMEM((2, S, HD), BF16),
            pltpu.VMEM((2, S, HD), BF16),
            pltpu.VMEM((S // KB, C, KB), F32),
            pltpu.VMEM((2, 2, C, HD), BF16),
            pltpu.VMEM((2, C, HD), BF16),
            pltpu.VMEM((C, 2 * FL), BF16),
            pltpu.VMEM((RING, C, D), BF16),
            pltpu.VMEM((RING, C // 2, D), BF16),
            pltpu.VMEM((RING, C // 2, D), BF16),
            pltpu.VMEM((RING, C // 2, D), BF16),
            pltpu.VMEM((RING, C // 4, D), BF16),
            dma((12, RING)),
            dma((RING,)),
            dma((7,)),
            dma((2, 4)),
            dma((2, 2)),
            dma((n,)),
            dma((2,)),
            dma((14,)),
            dma((11,)),
            dma((11,)),
            dma((11,)),
            dma((29,)),
        ],
        compiler_params=pltpu.CompilerParams(collective_id=0, has_side_effects=True, vmem_limit_bytes=66_000_000),
        name="layers",
    )(
        hidden, lengths, w_query.reshape(L, D, HD), w_key.reshape(L, D, HD), w_value.reshape(L, D, HD),
        w_out.reshape(L, HD, D), w_gate, w_up, w_down, norm_attn, norm_mlp, jnp.asarray(rope_table(S, HD)),
    )
    h, kc, vc = outs[:3]
    return h, kc.reshape(L, B, 1, S, HD), vc.reshape(L, B, 1, S, HD)


def solution(mesh):
    head_cols = P(None, None, "tp", None)
    head_rows = P(None, "tp", None, None)
    ff_cols = P(None, None, "tp")
    ff_rows = P(None, "tp", None)
    return jax.shard_map(
        run_layers,
        mesh=mesh,
        in_specs=(P("dp"), P("dp"), head_cols, head_cols, head_cols, head_rows, ff_cols, ff_cols, ff_rows, P(), P()),
        out_specs=(P("dp"), P(None, "dp", "tp"), P(None, "dp", "tp")),
        check_vma=False,
    )
```

time: 1520 us -> 521 us (0.34)
  waiting for transfers between devices: 1180 us -> 0 us
  Pallas kernels: 0 us -> 502 us
  matrix products: 204 us -> 0 us
  other arithmetic: 88 us -> 0 us
    psum x4 -> x0, waiting for transfers between devices: 1180 us -> none  [shard_body(): summed = lax.psum(part_sum, 'tp')]
    pallas_call x0 -> x1, Pallas kernels: none -> 502 us  [run_layers(): pl.pallas_call(functools.partial(layers_kernel, C), out_shape=[jax.ShapeD...]
    dot_general x14 -> x0, matrix products: 165 us -> none  [the longest x2 36.7 us: shard_body(): jnp.einsum('bqhd,hdm->bqm', attn_out, w_out[layer_idx], preferred_element...]
    reduce_sum x4 -> x0, other arithmetic: 51.3 us -> none  [rms_norm(): mean_sq = jnp.mean(x_f32 * x_f32, axis=-1, keepdims=True)]
    sub x2 -> x0, matrix products: 39.2 us -> none  [attention(): attn_probs = jax.nn.softmax(scores, axis=-1).astype(jnp.bfloat16)]
    convert_element_type x1 -> x0, other arithmetic: 19.8 us -> none  [shard_body(): (hidden_state.astype(jnp.float32) + summed.astype(jnp.float32)).astype(jn...]
  transfers between devices with their start and end apart: 4 -> 0, of which waited for: 4 -> 0; matrix products, arithmetic and copies ran while one was open for 0% -> 0% of each run, Pallas kernels for 0% -> 0%
where the time goes in v1:
time: 521 us
  Pallas kernels  502 us (96%)
  local copies, waits for them, and re-layouts  18 us (3%)
    pallas_call x1, Pallas kernels, run_layers(): pl.pallas_call(functools.partial(layers_kernel, C), out_shape=[jax.ShapeD...  502 us
    unnamed x7, local copies, waits for them, and re-layouts  18 us

profile of v1, /device:TPU:0, one launch (start us, length us, event | category | flops | bytes accessed | tf_op | source)
XLA Modules:
  0.0 521.1 jit_solution(3174881440356485476)
XLA Ops:
  0.6 502.4 %layers.1 = (bf16[2,2048,2048]{2,1,0:T(8,128)(2,1)}, bf16[2,2,2048,128]{3,2,1,0:T(8,128)(2,1)}, bf16[2,2,2048,128]{3,2,1,0:T(8,128)(2,1)}, bf16[2048,128]{1,0:T(...) custom-call(bf16[2,2048,2048]{2,1,0:T(8,128)(2,1)} %hid.1, ...), custom_call_target="tpu_custom_call" | custom-call | tf_op jit(solution)/shard_map/layers/pallas_call | solution.py:568
  503.1 0.0 copy-start.1
  503.1 14.3 %copy.20 = bf16[2,2048,2048]{2,1,0:T(8,128)(2,1)} copy(bf16[2,2048,2048]{2,1,0:T(8,128)(2,1)} %get-tuple-element.15) | data formatting | bytes 33554432
  517.4 0.0 copy-done.1
  517.4 0.0 copy-start
  517.4 1.3 copy.21
  518.7 1.0 copy-done
  519.7 1.3 copy.22
Async XLA Ops:
  503.1 14.3 %copy-start.1 = (bf16[2,2,2048,128]{3,2,1,0:T(8,128)(2,1)S(1)}, bf16[2,2,2048,128]{3,2,1,0:T(8,128)(2,1)}, u32[]{:S(2)}) copy-start(bf16[2,2,2048,128]{3,2,1,0:T(8,128)(2,1)} %get-tuple-element.7) | copy-start | bytes 6291460
  517.4 2.3 copy-start

commit v2 on v1

--- a/solution.py
+++ b/solution.py
@@ -12,6 +12,8 @@
 ROPE_BASE = 10000.0
 CHUNK = 128
 RING = 8
+EXCHANGE, FINISH, PASS, SHARE, RETIRE, FORWARD = 1, 3, 4, 5, 6, 7
+AHEAD = 2
 F32 = jnp.float32
 BF16 = jnp.bfloat16
 MESH = pl.DeviceIdType.MESH
@@ -35,7 +37,7 @@
     n = S // C
     H2, H4 = C // 2, C // 4
     NB = RING
-    KB = sc.shape[2]
+    KB = sc.shape[3]
     RB = 16
 
     dp = lax.axis_index("dp")
@@ -72,15 +74,12 @@
 
     lcopy = pltpu.make_async_copy
 
-    tensors = [(wo, 0, lo.at[0], HD, 1), (wg, 0, lg.at[0], D, 4), (wu, 0, lu.at[0], D, 4), (wd, 0, ld.at[0], FL, 4),
+    tensors = [(wo, 0, lo.at[0], HD, 4), (wg, 0, lg.at[0], D, 4), (wu, 0, lu.at[0], D, 4), (wd, 0, ld.at[0], FL, 4),
                (wq, 1, lq, D, 1), (wk, 1, lk, D, 1), (wv, 1, lv, D, 1), (wo, 1, lo.at[1], HD, 1),
                (wg, 1, lg.at[1], D, 4), (wu, 1, lu.at[1], D, 4), (wd, 1, ld.at[1], FL, 4)]
     first = [0]
     for t in tensors:
         first.append(first[-1] + t[4])
-    pieces = first[-1]
-    rate = 16 // n if n < 16 else 1
-    lead = 3
 
     def part_rows(t, part):
         half = tensors[t][3] // 2
@@ -119,21 +118,23 @@
         return lcopy(src, dst, s_wl.at[i])
 
     def base(k):
-        return pl.multiple_of(lax.rem(k, n) * C, C)
+        return pl.multiple_of(lax.rem(k + 2 * n, n) * C, C)
 
     def ch(i, k):
-        return s_ch.at[i, lax.rem(k, NB)]
+        return s_ch.at[i, lax.rem(k + 2 * NB, NB)]
 
     def h_d2d(k):
-        kk = lax.rem(k, NB)
+        kk = lax.rem(k + 2 * NB, NB)
         return rcopy(pb.at[kk, pl.ds(his, H2)], d2d.at[kk], ch(0, k), ch(1, k), sib)
 
-    def h_up(k):
-        kk = lax.rem(k, NB)
-        return rcopy(ts.at[kk], ro.at[kk], ch(2, k), ch(3, k), inward)
+    def h_up(k, second):
+        kk = lax.rem(k + 2 * NB, NB)
+        rows = pl.ds(off_b if second else off_a, H4)
+        i = 12 if second else 2
+        return rcopy(ts.at[kk, rows], ro.at[kk, rows], ch(i, k), ch(i + 1, k), inward)
 
     def h_mid(k):
-        kk = lax.rem(k, NB)
+        kk = lax.rem(k + 2 * NB, NB)
         return rcopy(ts.at[kk, pl.ds(0, H4)], ri.at[kk], ch(4, k), ch(5, k), inward)
 
     def rows_of(k, off, size):
@@ -155,10 +156,10 @@
         return pl.ds(pl.multiple_of(base(k) + my, H2), H2)
 
     def h_yh(k):
-        return rcopy(rows_of(k, 0, H2), h.at[y, out_rows(k)], s_one.at[0], s_yh.at[lax.rem(k, NB)], ypart)
+        return rcopy(rows_of(k, 0, H2), h.at[y, out_rows(k)], s_one.at[0], s_yh.at[lax.rem(k + 2 * NB, NB)], ypart)
 
     def h_yh_recv(k):
-        return rcopy(rows_of(k, 0, H2), h.at[1 - y, out_rows(k)], s_one.at[0], s_yh.at[lax.rem(k, NB)], ypart)
+        return rcopy(rows_of(k, 0, H2), h.at[1 - y, out_rows(k)], s_one.at[0], s_yh.at[lax.rem(k + 2 * NB, NB)], ypart)
 
     def h_hs(k):
         return rcopy(h.at[1 - y, out_rows(k)], h.at[1 - y, out_rows(k)], s_one.at[1], s_one.at[2], sib)
@@ -204,7 +205,7 @@
                 kv_copy(1, which, na, 0, 0, True).wait_send()
 
     def o_copy(na):
-        par = lax.rem(na, 2)
+        par = lax.rem(na, 4)
         return rcopy(osend.at[par], ob.at[par, 1], s_o.at[0, par], s_o.at[1, par], ypart)
 
     def xo_load(i):
@@ -226,7 +227,8 @@
         layer = stage // 2
         i = u - stage * n
         na = layer * n + i
-        par = lax.rem(na, 2)
+        par = lax.rem(na, 4)
+        xpar = lax.rem(i, 2)
         r0 = pl.multiple_of(i * C, C)
 
         @pl.when(na >= 2)
@@ -244,7 +246,7 @@
             def _():
                 xo_load(i + 1).start()
 
-            norm(lambda r: xo[par, r:r + RB, :], a_write(1), gain)
+            norm(lambda r: xo[xpar, r:r + RB, :], a_write(1), gain)
 
         norm(x_chunk(r0), a_write(0), gain)
 
@@ -257,12 +259,12 @@
         def rot(v):
             return v * cos_t + pltpu.roll(v, HD // 2, 1) * sin_t
 
-        blocks = (i * C + C + KB - 1) // KB
-        for j in (1, 0):
+        queries = []
+        for j in (0, 1):
             aj = 0 if j == 0 else 1 - layer
             wj = 0 if j == 0 else layer
             qkv = jnp.dot(a[aj], wqkv[wj], preferred_element_type=F32)
-            q = (rot(qkv[:, 0:HD]) * HD ** -0.5).astype(BF16)
+            queries.append((rot(qkv[:, 0:HD]) * HD ** -0.5).astype(BF16))
             kb[j, pl.ds(r0, C), :] = rot(qkv[:, HD:2 * HD]).astype(BF16)
             vb[j, pl.ds(r0, C), :] = qkv[:, 2 * HD:3 * HD].astype(BF16)
             for which in range(2):
@@ -277,54 +279,67 @@
                     def _(which=which):
                         kv_copy(1, which, na, 1, i, True).start()
 
-            length = lens[y if j == 0 else y * layer + (1 - y) * (1 - layer)]
-            limit = jnp.minimum(lax.broadcasted_iota(jnp.int32, (C, KB), 0) + (r0 + 1), length)
+        @pl.when((na >= 4) & (na < n + 4))
+        def _():
+            o_copy(na - 4).wait_send()
+
+        lengths = (lens[y], lens[y * layer + (1 - y) * (1 - layer)])
+
+        def attend(blocks):
+            rows = lax.broadcasted_iota(jnp.int32, (C, KB), 0) + (r0 + 1)
             cols = lax.broadcasted_iota(jnp.int32, (C, KB), 1)
-
-            def scores(b, m, j=j, q=q, limit=limit, cols=cols):
-                keys = kb[j, pl.ds(pl.multiple_of(b * KB, KB), KB), :]
-                s = lax.dot_general(q, keys, (((1,), (1,)), ((), ())), preferred_element_type=F32)
-                s = jnp.where(cols + b * KB < limit, s, -1e30)
-                sc[b] = s
-                return jnp.maximum(m, lanes(jnp.maximum, s))
-
-            m = lax.fori_loop(0, blocks, scores, jnp.full((C, 128), -1e30, F32))
-            m = jnp.max(m, axis=1, keepdims=True)
-
-            def exps(b, l, m=m):
-                e = jnp.exp(sc[b] - m)
-                sc[b] = e
-                return l + lanes(jnp.add, e)
-
-            l = lax.fori_loop(0, blocks, exps, jnp.zeros((C, 128), F32))
-            inv = 1.0 / jnp.sum(l, axis=1, keepdims=True)
-
-            def mix(b, o, j=j, inv=inv):
-                p = (sc[b] * inv).astype(BF16)
-                return o + jnp.dot(p, vb[j, pl.ds(pl.multiple_of(b * KB, KB), KB), :], preferred_element_type=F32)
-
-            o = lax.fori_loop(0, blocks, mix, jnp.zeros((C, HD), F32)).astype(BF16)
-            if j == 0:
-                ob[par, 0] = o
-            else:
-                @pl.when(layer == 0)
-                def _(o=o):
-                    @pl.when(i >= 2)
-                    def _():
-                        o_copy(na - 2).wait_send()
-
-                    osend[par] = o
-                    o_copy(na).start()
-
-                @pl.when(layer == 1)
-                def _(o=o):
-                    ob[par, 1] = o
+            tops = []
+            for j in (0, 1):
+                top = None
+                for b in range(blocks):
+                    keys = kb[j, b * KB:(b + 1) * KB, :]
+                    s = lax.dot_general(queries[j], keys, (((1,), (1,)), ((), ())), preferred_element_type=F32)
+                    limit = lengths[j] - b * KB
+                    if b == blocks - 1:
+                        limit = jnp.minimum(rows - b * KB, limit)
+                    s = jnp.where(cols < limit, s, -1e30)
+                    sc[j, b] = s
+                    s = lanes(jnp.maximum, s)
+                    top = s if top is None else jnp.maximum(top, s)
+                tops.append(jnp.max(top, axis=1, keepdims=True))
+            invs = []
+            for j in (0, 1):
+                total = None
+                for b in range(blocks):
+                    e = jnp.exp(sc[j, b] - tops[j])
+                    sc[j, b] = e
+                    e = lanes(jnp.add, e)
+                    total = e if total is None else total + e
+                invs.append(1.0 / jnp.sum(total, axis=1, keepdims=True))
+            for j in (0, 1):
+                o = None
+                for b in range(blocks):
+                    p = (sc[j, b] * invs[j]).astype(BF16)
+                    d = jnp.dot(p, vb[j, b * KB:(b + 1) * KB, :], preferred_element_type=F32)
+                    o = d if o is None else o + d
+                if j == 0:
+                    ob[par, 0] = o.astype(BF16)
+                else:
+                    osend[par] = o.astype(BF16)
+
+        for blocks in range(1, S // KB + 1):
+            @pl.when((i * C + C + KB - 1) // KB == blocks)
+            def _(blocks=blocks):
+                attend(blocks)
+
+        @pl.when(layer == 0)
+        def _():
+            o_copy(na).start()
+
+        @pl.when(layer == 1)
+        def _():
+            ob[par, 1] = osend[par]
 
     NBLK = min(512, D)
 
     def out_proj(s):
         layer = s // (2 * n)
-        par = lax.rem(layer * n + lax.rem(s, n), 2)
+        par = lax.rem(layer * n + lax.rem(s, n), 4)
 
         @pl.when(layer == 0)
         def _():
@@ -349,29 +364,33 @@
 
     def send_up(k):
         h_d2d(k).wait_recv()
-        kk = lax.rem(k, NB)
-        for r in range(0, H2, RB):
-            rr = pl.ds(pl.multiple_of(my + r, RB), RB)
-            ts[kk, r:r + RB, :] = (pb[kk, rr, :].astype(F32) + d2d[kk, r:r + RB, :].astype(F32)).astype(BF16)
-        h_up(k).start()
+        kk = lax.rem(k + 2 * NB, NB)
+        for second in (False, True):
+            off = off_b if second else off_a
+            for r in range(0, H4, RB):
+                rr = pl.ds(pl.multiple_of(off + r, RB), RB)
+                mine = pl.ds(pl.multiple_of(my + off + r, RB), RB)
+                ts[kk, rr, :] = (pb[kk, mine, :].astype(F32) + d2d[kk, rr, :].astype(F32)).astype(BF16)
+            h_up(k, second).start()
 
     def part(k, off, r):
-        kk = lax.rem(k, NB)
+        kk = lax.rem(k + 2 * NB, NB)
         mine = pl.ds(pl.multiple_of(my + off + r, RB), RB)
         rr = pl.ds(pl.multiple_of(off + r, RB), RB)
         return pb[kk, mine, :].astype(F32) + d2d[kk, rr, :].astype(F32) + ro[kk, rr, :].astype(F32)
 
     def exchange(k):
         h_d2d(k).wait_recv()
-        h_up(k).wait_recv()
-        kk = lax.rem(k, NB)
+        h_up(k, False).wait_recv()
+        kk = lax.rem(k + 2 * NB, NB)
         for r in range(0, H4, RB):
             ts[kk, r:r + RB, :] = part(k, off_a, r).astype(BF16)
         h_mid(k).start()
 
     def finish(k):
+        h_up(k, True).wait_recv()
         h_mid(k).wait_recv()
-        kk = lax.rem(k, NB)
+        kk = lax.rem(k + 2 * NB, NB)
         for r in range(0, H4, RB):
             rows = pl.ds(pl.multiple_of(base(k) + my + off_b + r, RB), RB)
             total = part(k, off_b, r) + ri[kk, r:r + RB, :].astype(F32)
@@ -406,7 +425,8 @@
 
         @pl.when(outer)
         def _():
-            h_up(k).wait_send()
+            h_up(k, False).wait_send()
+            h_up(k, True).wait_send()
 
         @pl.when(inner)
         def _():
@@ -428,15 +448,14 @@
             ok = ok & cond
         pl.when(ok)(lambda: what(k))
 
-    over_y(0, 0).start()
+    for p in range(tensors[0][4]):
+        over_y(0, p).start()
     x_load(0).start()
     xo_load(0).start()
     rope_copy = lcopy(rope, ropev, s_one.at[6])
     rope_copy.start()
     for i in (0, 1, 2, 3):
         load(i, 0).start()
-    for p in range(1, lead):
-        over_y(1, p - 1).start()
     for i in range(1, n):
         x_load(i).start()
     for i in (4, 5, 6):
@@ -450,7 +469,11 @@
         load(i, 0).wait()
 
     def slot(s, carry):
-        at(s - 5, retire)
+        at(s - RETIRE, retire)
+        at(s - SHARE, share, outer)
+        at(s - PASS, pass_on, inner)
+        at(s - FINISH, finish, inner)
+        at(s - FORWARD, forward_out, s - FORWARD >= 3 * n)
 
         @pl.when(s == n)
         def _():
@@ -462,7 +485,7 @@
             for i in (4, 5, 6, 11, 12, 13):
                 load(i, 1).wait()
 
-        @pl.when(s == 2 * n - 1)
+        @pl.when(s == 2 * n - AHEAD)
         def _():
             for i in (0, 1, 2, 3, 7, 8, 9, 10):
                 load(i, 1).wait()
@@ -480,39 +503,43 @@
 
         at(s, lambda k: h_d2d(k).start())
 
-        u = s + 1
+        u = s + AHEAD
 
         @pl.when((u < n) | ((u >= 2 * n) & (u < 3 * n)))
         def _():
             attn(u)
 
-        at(s - 4, share, outer)
-        at(s - 3, pass_on, inner)
-        at(s - 2, finish, inner)
-        at(s - 1, exchange, inner)
+        at(s - EXCHANGE, exchange, inner)
         at(s, send_up, outer)
-        at(s - 6, forward_out, s - 6 >= 3 * n)
+
+        @pl.when(s == -AHEAD)
+        def _():
+            for p in range(2):
+                over_y(1, p).start()
 
         @pl.when(s == -1)
         def _():
-            over_y(0, 0).wait_recv()
-            over_x(0, 0).start()
+            for p in range(tensors[0][4]):
+                over_y(0, p).wait_recv()
+                over_x(0, p).start()
             wait_xr(0)
             load(10, 0).start()
             load(3, 0).wait()
             load(10, 0).wait()
 
-        for r in range(rate):
+        for r in range(max(1, 16 // n)):
+            beat = s * 16 // n + r
+            on_beat = (s >= 0) & (lax.rem(s, max(1, n // 16)) == 0)
             for t in range(1, len(tensors)):
-                p = s * rate + r + lead - first[t]
-
-                @pl.when((s >= 0) & (p >= 0) & (p < tensors[t][4]))
+                p = beat + 2 - (first[t] - first[1])
+
+                @pl.when(on_beat & (p >= (2 if t == 1 else 0)) & (p < tensors[t][4]))
                 def _(t=t, p=p):
                     over_y(t, p).start()
 
-                q = s * rate + r - first[t]
-
-                @pl.when((s >= 0) & (q >= 0) & (q < tensors[t][4]))
+                q = beat - 2 - (first[t] - first[1])
+
+                @pl.when(on_beat & (q >= 0) & (q < tensors[t][4]))
                 def _(t=t, q=q):
                     over_y(t, q).wait_recv()
                     over_x(t, q).start()
@@ -539,12 +566,10 @@
 
         return carry
 
-    lax.fori_loop(-1, 4 * n + 6, slot, 0)
+    lax.fori_loop(0, 4 * n + FORWARD + AHEAD, lambda t, carry: slot(t - AHEAD, carry), 0)
 
     for t in range(len(tensors)):
         wait_sends(t)
-    for na in (n - 2, n - 1):
-        o_copy(na).wait_send()
     for na in (2 * n - 2, 2 * n - 1):
         kv_wait(na)
     for which, out in ((0, kc), (1, vc)):
@@ -561,7 +586,7 @@
     FL = w_gate.shape[2]
     C = CHUNK
     n = S // C
-    KB = min(256, S)
+    KB = min(512, S // 4)
     any_space = pl.BlockSpec(memory_space=pl.ANY)
     vmem = pl.BlockSpec(memory_space=pltpu.VMEM)
     dma = pltpu.SemaphoreType.DMA
@@ -593,27 +618,27 @@
             pltpu.VMEM((S, HD), F32),
             pltpu.VMEM((2, S, HD), BF16),
             pltpu.VMEM((2, S, HD), BF16),
-            pltpu.VMEM((S // KB, C, KB), F32),
-            pltpu.VMEM((2, 2, C, HD), BF16),
-            pltpu.VMEM((2, C, HD), BF16),
+            pltpu.VMEM((2, S // KB, C, KB), F32),
+            pltpu.VMEM((4, 2, C, HD), BF16),
+            pltpu.VMEM((4, C, HD), BF16),
             pltpu.VMEM((C, 2 * FL), BF16),
             pltpu.VMEM((RING, C, D), BF16),
             pltpu.VMEM((RING, C // 2, D), BF16),
             pltpu.VMEM((RING, C // 2, D), BF16),
             pltpu.VMEM((RING, C // 2, D), BF16),
             pltpu.VMEM((RING, C // 4, D), BF16),
-            dma((12, RING)),
+            dma((14, RING)),
             dma((RING,)),
             dma((7,)),
             dma((2, 4)),
-            dma((2, 2)),
+            dma((2, 4)),
             dma((n,)),
             dma((2,)),
             dma((14,)),
             dma((11,)),
             dma((11,)),
             dma((11,)),
-            dma((29,)),
+            dma((32,)),
         ],
         compiler_params=pltpu.CompilerParams(collective_id=0, has_side_effects=True, vmem_limit_bytes=66_000_000),
         name="layers",

time: 521 us -> 435 us (0.83)
  Pallas kernels: 502 us -> 416 us
    pallas_call x1, Pallas kernels: 502 us -> 416 us  [run_layers(): pl.pallas_call(functools.partial(layers_kernel, C), out_shape=[jax.ShapeD...]
where the time goes in v2:
time: 435 us; the launch traced here: 434 us
  Pallas kernels  416 us (96%)
  local copies, waits for them, and re-layouts  18 us (4%)
    pallas_call x1, Pallas kernels, run_layers(): pl.pallas_call(functools.partial(layers_kernel, C), out_shape=[jax.ShapeD...  416 us
    unnamed x7, local copies, waits for them, and re-layouts  18 us

profile of v2, /device:TPU:0, one launch (start us, length us, event | category | flops | bytes accessed | tf_op | source)
XLA Modules:
  0.0 434.4 jit_solution(1905759365099839046)
XLA Ops:
  0.6 415.7 %layers.1 = (bf16[2,2048,2048]{2,1,0:T(8,128)(2,1)}, bf16[2,2,2048,128]{3,2,1,0:T(8,128)(2,1)}, bf16[2,2,2048,128]{3,2,1,0:T(8,128)(2,1)}, bf16[2048,128]{1,0:T(...) custom-call(bf16[2,2048,2048]{2,1,0:T(8,128)(2,1)} %hid.1, ...), custom_call_target="tpu_custom_call" | custom-call | tf_op jit(solution)/shard_map/layers/pallas_call | solution.py:593
  416.4 0.0 copy-start.1
  416.4 14.3 %copy.20 = bf16[2,2048,2048]{2,1,0:T(8,128)(2,1)} copy(bf16[2,2048,2048]{2,1,0:T(8,128)(2,1)} %get-tuple-element.15) | data formatting | bytes 33554432
  430.7 0.0 copy-done.1
  430.7 0.0 copy-start
  430.7 1.3 copy.21
  432.0 1.0 copy-done
  433.0 1.3 copy.22
Async XLA Ops:
  416.4 14.3 %copy-start.1 = (bf16[2,2,2048,128]{3,2,1,0:T(8,128)(2,1)S(1)}, bf16[2,2,2048,128]{3,2,1,0:T(8,128)(2,1)}, u32[]{:S(2)}) copy-start(bf16[2,2,2048,128]{3,2,1,0:T(8,128)(2,1)} %get-tuple-element.7) | copy-start | bytes 6291460
  430.7 2.3 copy-start

commit v3 on v2

--- a/solution.py
+++ b/solution.py
@@ -12,7 +12,9 @@
 ROPE_BASE = 10000.0
 CHUNK = 128
 RING = 8
-EXCHANGE, FINISH, PASS, SHARE, RETIRE, FORWARD = 1, 3, 4, 5, 6, 7
+EXCHANGE, FINISH, PASS, SHARE_B, SHARE_A, RETIRE, FORWARD = 1, 2, 4, 4, 5, 6, 7
+(D2D_S, D2D_R, UP_S, UP_A0, UP_A1, UP_B, MID_S, MID_0, MID_1, FI_S, FI_0, FI_1,
+ FO_S, FO_B, FO_A0, FO_A1, FS_S, FS_R) = range(18)
 AHEAD = 2
 F32 = jnp.float32
 BF16 = jnp.bfloat16
@@ -27,23 +29,24 @@
     return np.concatenate([np.cos(angles), np.sin(angles)], axis=-1).astype(np.float32)
 
 
-def layers_kernel(C, hid, lens, wq, wk, wv, wo, wg, wu, wd, ga, gm, rope,
+def layers_kernel(C, hid, lens_in, wq, wk, wv, wo, wg, wu, wd, ga_in, gm_in, rope,
                   h, kc, vc, lq, lk, lv, lo, lg, lu, ld,
-                  x, xo, a, wqkv, wov, wgv, wuv, wdv, ropev, kb, vb, sc, ob, osend, mb, pb, d2d, ts, ro, ri,
-                  s_ch, s_yh, s_one, s_kv, s_o, s_x, s_xo, s_wl, s_ys, s_xs, s_xr, s_yr):
-    S, D = x.shape
+                  lens, ga, gm, xo, a, wqkv, wov, wgv, wuv, wdv, ropev, kb, vb, sc, ob, osend, mb, pb, d2d, ts, ro, ri,
+                  s_ch, s_yh, s_one, s_kv, s_o, s_x, s_xo, s_rope, s_wl, s_ys, s_xs, s_xr, s_yr):
+    _, S, D = hid.shape
     HD = wq.shape[2]
     FL = wg.shape[2]
     n = S // C
-    H2, H4 = C // 2, C // 4
+    H2, H4, H8 = C // 2, C // 4, C // 8
     NB = RING
     KB = sc.shape[3]
-    RB = 16
+    RB = min(16, H8)
 
     dp = lax.axis_index("dp")
     tp = lax.axis_index("tp")
     c = lax.rem(tp, 2)
     y = lax.rem(tp // 2, 2)
+    x = h.at[y]
     z = tp // 4
     left = z < 2
     inner = (z == 1) | (z == 2)
@@ -74,8 +77,8 @@
 
     lcopy = pltpu.make_async_copy
 
-    tensors = [(wo, 0, lo.at[0], HD, 4), (wg, 0, lg.at[0], D, 4), (wu, 0, lu.at[0], D, 4), (wd, 0, ld.at[0], FL, 4),
-               (wq, 1, lq, D, 1), (wk, 1, lk, D, 1), (wv, 1, lv, D, 1), (wo, 1, lo.at[1], HD, 1),
+    tensors = [(wo, 0, wov.at[pl.ds(HD, HD)], HD, 4), (wg, 0, lg.at[0], D, 4), (wu, 0, lu.at[0], D, 4), (wd, 0, ld.at[0], FL, 4),
+               (wq, 1, lq, D, 1), (wk, 1, lk, D, 1), (wv, 1, lv, D, 1), (wo, 1, lo, HD, 1),
                (wg, 1, lg.at[1], D, 4), (wu, 1, lu.at[1], D, 4), (wd, 1, ld.at[1], FL, 4)]
     first = [0]
     for t in tensors:
@@ -112,7 +115,7 @@
         if j == 0:
             src = (wq, wk, wv, wo, wg, wu, wd)[kind].at[layer]
         else:
-            src = (lq, lk, lv, lo.at[layer], lg.at[layer], lu.at[layer], ld.at[layer])[kind]
+            src = (lq, lk, lv, lo, lg.at[layer], lu.at[layer], ld.at[layer])[kind]
         dst = (wqkv.at[j, :, pl.ds(0, HD)], wqkv.at[j, :, pl.ds(HD, HD)], wqkv.at[j, :, pl.ds(2 * HD, HD)],
                wov.at[pl.ds(j * HD, HD)], wgv.at[j], wuv.at[j], wdv.at[pl.ds(j * FL, FL)])[kind]
         return lcopy(src, dst, s_wl.at[i])
@@ -123,50 +126,44 @@
     def ch(i, k):
         return s_ch.at[i, lax.rem(k + 2 * NB, NB)]
 
+    def slot_of(k):
+        return lax.rem(k + 2 * NB, NB)
+
     def h_d2d(k):
-        kk = lax.rem(k + 2 * NB, NB)
-        return rcopy(pb.at[kk, pl.ds(his, H2)], d2d.at[kk], ch(0, k), ch(1, k), sib)
-
-    def h_up(k, second):
-        kk = lax.rem(k + 2 * NB, NB)
-        rows = pl.ds(off_b if second else off_a, H4)
-        i = 12 if second else 2
-        return rcopy(ts.at[kk, rows], ro.at[kk, rows], ch(i, k), ch(i + 1, k), inward)
-
-    def h_mid(k):
-        kk = lax.rem(k + 2 * NB, NB)
-        return rcopy(ts.at[kk, pl.ds(0, H4)], ri.at[kk], ch(4, k), ch(5, k), inward)
+        kk = slot_of(k)
+        return rcopy(pb.at[kk, pl.ds(his, H2)], d2d.at[kk], ch(D2D_S, k), ch(D2D_R, k), sib)
+
+    def h_up(k, off, size, recv):
+        kk = slot_of(k)
+        rows = pl.ds(pl.multiple_of(off, H8), size)
+        return rcopy(ts.at[kk, rows], ro.at[kk, rows], ch(UP_S, k), ch(recv, k), inward)
+
+    def h_mid(k, half):
+        kk = slot_of(k)
+        rows = pl.ds(half * H8, H8)
+        return rcopy(ts.at[kk, rows], ri.at[kk, rows], ch(MID_S, k), ch(MID_0 + half, k), inward)
+
+    def out_rows(k, off, size):
+        return pl.ds(pl.multiple_of(base(k) + my + off, H8), size)
 
     def rows_of(k, off, size):
-        return x.at[pl.ds(pl.multiple_of(base(k) + my + off, H4), size)]
-
-    def h_fi(k):
-        return rcopy(rows_of(k, off_b, H4), rows_of(k, off_b, H4), ch(6, k), ch(7, k), inward)
-
-    def h_fo(k, off, size):
-        return rcopy(rows_of(k, off, size), rows_of(k, off, size), ch(8, k), ch(9, k), outward)
-
-    def h_fo_recv(k):
-        return rcopy(rows_of(k, 0, H2), rows_of(k, 0, H2), ch(8, k), ch(9, k), inward)
-
-    def h_fs(k):
-        return rcopy(rows_of(k, 0, H2), rows_of(k, 0, H2), ch(10, k), ch(11, k), sib)
-
-    def out_rows(k):
-        return pl.ds(pl.multiple_of(base(k) + my, H2), H2)
-
-    def h_yh(k):
-        return rcopy(rows_of(k, 0, H2), h.at[y, out_rows(k)], s_one.at[0], s_yh.at[lax.rem(k + 2 * NB, NB)], ypart)
-
-    def h_yh_recv(k):
-        return rcopy(rows_of(k, 0, H2), h.at[1 - y, out_rows(k)], s_one.at[0], s_yh.at[lax.rem(k + 2 * NB, NB)], ypart)
+        return x.at[out_rows(k, off, size)]
+
+    def h_fi(k, off, recv, size):
+        return rcopy(rows_of(k, off, size), rows_of(k, off, size), ch(FI_S, k), ch(recv, k), inward)
+
+    def h_fo(k, off, recv, size, dev):
+        return rcopy(rows_of(k, off, size), rows_of(k, off, size), ch(FO_S, k), ch(recv, k), dev)
+
+    def h_fs(k, off, size):
+        return rcopy(rows_of(k, off, size), rows_of(k, off, size), ch(FS_S, k), ch(FS_R, k), sib)
+
+    def h_yh(k, off, size):
+        return rcopy(rows_of(k, off, size), rows_of(k, off, size), s_one.at[0], s_yh.at[lax.rem(k + 2 * n, n)], ypart)
 
     def h_hs(k):
-        return rcopy(h.at[1 - y, out_rows(k)], h.at[1 - y, out_rows(k)], s_one.at[1], s_one.at[2], sib)
-
-    def h_local(k):
-        rows = pl.ds(base(k), C)
-        return lcopy(x.at[rows], h.at[y, rows], s_one.at[3])
+        rows = out_rows(k, 0, H2)
+        return rcopy(h.at[1 - y, rows], h.at[1 - y, rows], s_one.at[1], s_one.at[2], sib)
 
     def norm(read, write, gain):
         for r in range(0, C, RB):
@@ -214,7 +211,11 @@
 
     def x_load(i):
         rows = pl.ds(pl.multiple_of(i * C, C), C)
-        return lcopy(hid.at[y, rows], x.at[rows], s_x.at[i])
+        return lcopy(hid.at[y, rows], x.at[rows], s_x.at[lax.rem(i, 2)])
+
+    def rope_load(i):
+        rows = pl.ds(pl.multiple_of(i * C, C), C)
+        return lcopy(rope.at[rows], ropev.at[rows], s_rope.at[lax.rem(i, 2)])
 
     def lanes(op, v):
         out = v[:, 0:128]
@@ -241,10 +242,13 @@
         def _():
             x_load(i).wait()
             xo_load(i).wait()
+            rope_load(i).wait()
 
             @pl.when(i + 1 < n)
             def _():
+                x_load(i + 1).start()
                 xo_load(i + 1).start()
+                rope_load(i + 1).start()
 
             norm(lambda r: xo[xpar, r:r + RB, :], a_write(1), gain)
 
@@ -364,82 +368,98 @@
 
     def send_up(k):
         h_d2d(k).wait_recv()
-        kk = lax.rem(k + 2 * NB, NB)
-        for second in (False, True):
-            off = off_b if second else off_a
-            for r in range(0, H4, RB):
-                rr = pl.ds(pl.multiple_of(off + r, RB), RB)
-                mine = pl.ds(pl.multiple_of(my + off + r, RB), RB)
-                ts[kk, rr, :] = (pb[kk, mine, :].astype(F32) + d2d[kk, rr, :].astype(F32)).astype(BF16)
-            h_up(k, second).start()
+        kk = slot_of(k)
+        for off, recvs in ((off_a, (UP_A0, UP_A1)), (off_b, (UP_B, UP_B))):
+            for half in (0, 1):
+                for r in range(half * H8, half * H8 + H8, RB):
+                    rr = pl.ds(pl.multiple_of(off + r, RB), RB)
+                    mine = pl.ds(pl.multiple_of(my + off + r, RB), RB)
+                    ts[kk, rr, :] = (pb[kk, mine, :].astype(F32) + d2d[kk, rr, :].astype(F32)).astype(BF16)
+                h_up(k, off + half * H8, H8, recvs[half]).start()
 
     def part(k, off, r):
-        kk = lax.rem(k + 2 * NB, NB)
+        kk = slot_of(k)
         mine = pl.ds(pl.multiple_of(my + off + r, RB), RB)
         rr = pl.ds(pl.multiple_of(off + r, RB), RB)
         return pb[kk, mine, :].astype(F32) + d2d[kk, rr, :].astype(F32) + ro[kk, rr, :].astype(F32)
 
     def exchange(k):
         h_d2d(k).wait_recv()
-        h_up(k, False).wait_recv()
-        kk = lax.rem(k + 2 * NB, NB)
-        for r in range(0, H4, RB):
-            ts[kk, r:r + RB, :] = part(k, off_a, r).astype(BF16)
-        h_mid(k).start()
-
-    def finish(k):
-        h_up(k, True).wait_recv()
-        h_mid(k).wait_recv()
-        kk = lax.rem(k + 2 * NB, NB)
-        for r in range(0, H4, RB):
-            rows = pl.ds(pl.multiple_of(base(k) + my + off_b + r, RB), RB)
-            total = part(k, off_b, r) + ri[kk, r:r + RB, :].astype(F32)
-            x[rows, :] = (x[rows, :].astype(F32) + total).astype(BF16)
-        h_fi(k).start()
-        h_fo(k, off_b, H4).start()
+        kk = slot_of(k)
+        for half in (0, 1):
+            h_up(k, off_a, H8, UP_A0 + half).wait_recv()
+            for r in range(half * H8, half * H8 + H8, RB):
+                ts[kk, r:r + RB, :] = part(k, off_a, r).astype(BF16)
+            h_mid(k, half).start()
 
     def last_stage(k):
         return k >= 3 * n
 
+    def finish(k):
+        h_up(k, off_b, H4, UP_B).wait_recv()
+        kk = slot_of(k)
+        for half in (0, 1):
+            h_mid(k, half).wait_recv()
+            for r in range(half * H8, half * H8 + H8, RB):
+                rows = pl.ds(pl.multiple_of(base(k) + my + off_b + r, RB), RB)
+                total = part(k, off_b, r) + ri[kk, r:r + RB, :].astype(F32)
+                x[rows, :] = (x[rows, :].astype(F32) + total).astype(BF16)
+            h_fi(k, off_b + half * H8, FI_0 + half, H8).start()
+            h_fo(k, off_b + half * H8, FO_B, H8, outward).start()
+        h_fs(k, off_b, H4).start()
+
+        @pl.when(last_stage(k))
+        def _():
+            h_yh(k, off_b, H4).start()
+
     def pass_on(k):
-        h_fi(k).wait_recv()
-        h_fo(k, off_a, H4).start()
-        h_fs(k).start()
+        for half in (0, 1):
+            off = off_a + half * H8
+            h_fi(k, off, FI_0 + half, H8).wait_recv()
+            h_fo(k, off, FO_A0 + half, H8, outward).start()
+            h_fs(k, off, H8).start()
+
+            @pl.when(last_stage(k))
+            def _(off=off):
+                h_yh(k, off, H8).start()
+
+    def share_b(k):
+        h_fo(k, off_b, FO_B, H4, inward).wait_recv()
+        h_fs(k, off_b, H4).start()
 
         @pl.when(last_stage(k))
         def _():
-            h_yh(k).start()
-
-    def share(k):
-        h_fo_recv(k).wait_recv()
-        h_fs(k).start()
-
-        @pl.when(last_stage(k))
-        def _():
-            h_yh(k).start()
+            h_yh(k, off_b, H4).start()
+
+    def share_a(k):
+        for half in (0, 1):
+            off = off_a + half * H8
+            h_fo(k, off, FO_A0 + half, H8, inward).wait_recv()
+            h_fs(k, off, H8).start()
+
+            @pl.when(last_stage(k))
+            def _(off=off):
+                h_yh(k, off, H8).start()
 
     def retire(k):
-        h_fs(k).wait_recv()
-        h_fs(k).wait_send()
+        h_fs(k, 0, H2).wait_recv()
+        h_fs(k, 0, H2).wait_send()
         h_d2d(k).wait_send()
 
         @pl.when(outer)
         def _():
-            h_up(k, False).wait_send()
-            h_up(k, True).wait_send()
+            h_up(k, 0, H2, UP_B).wait_send()
 
         @pl.when(inner)
         def _():
-            h_mid(k).wait_send()
-            h_fi(k).wait_send()
-            h_fo(k, 0, H2).wait_send()
-
-        @pl.when(last_stage(k))
-        def _():
-            h_local(k).start()
+            kk = slot_of(k)
+            both = pl.ds(0, H4)
+            rcopy(ts.at[kk, both], ri.at[kk], ch(MID_S, k), ch(MID_0, k), inward).wait_send()
+            h_fi(k, off_b, FI_0, H4).wait_send()
+            h_fo(k, 0, FO_B, H2, outward).wait_send()
 
     def forward_out(k):
-        h_yh_recv(k).wait_recv()
+        h_yh(k, 0, H2).wait_recv()
         h_hs(k).start()
 
     def at(k, what, cond=None):
@@ -450,29 +470,29 @@
 
     for p in range(tensors[0][4]):
         over_y(0, p).start()
+    for i in (0, 1, 2):
+        load(i, 0).start()
     x_load(0).start()
     xo_load(0).start()
-    rope_copy = lcopy(rope, ropev, s_one.at[6])
-    rope_copy.start()
-    for i in (0, 1, 2, 3):
-        load(i, 0).start()
-    for i in range(1, n):
-        x_load(i).start()
-    for i in (4, 5, 6):
-        load(i, 0).start()
+    rope_load(0).start()
+    small = [lcopy(one, two, s_one.at[i]) for one, two, i in ((lens_in, lens, 3), (ga_in, ga, 6), (gm_in, gm, 7))]
+    for copy in small:
+        copy.start()
     for j in range(2):
         for r in range(0, S, KB):
             kb[j, r:r + KB, :] = jnp.zeros((KB, HD), BF16)
             vb[j, r:r + KB, :] = jnp.zeros((KB, HD), BF16)
-    rope_copy.wait()
     for i in (0, 1, 2):
         load(i, 0).wait()
+    load(3, 0).start()
+    for copy in small:
+        copy.wait()
 
     def slot(s, carry):
         at(s - RETIRE, retire)
-        at(s - SHARE, share, outer)
+        at(s - SHARE_A, share_a, outer)
+        at(s - SHARE_B, share_b, outer)
         at(s - PASS, pass_on, inner)
-        at(s - FINISH, finish, inner)
         at(s - FORWARD, forward_out, s - FORWARD >= 3 * n)
 
         @pl.when(s == n)
@@ -503,6 +523,7 @@
 
         at(s, lambda k: h_d2d(k).start())
 
+        at(s, send_up, outer & (s == 0))
         u = s + AHEAD
 
         @pl.when((u < n) | ((u >= 2 * n) & (u < 3 * n)))
@@ -510,12 +531,18 @@
             attn(u)
 
         at(s - EXCHANGE, exchange, inner)
-        at(s, send_up, outer)
+        at(s - FINISH, finish, inner)
+        at(s, send_up, outer & (s > 0))
 
         @pl.when(s == -AHEAD)
         def _():
             for p in range(2):
                 over_y(1, p).start()
+
+        @pl.when(s == 2)
+        def _():
+            for i in (4, 5, 6):
+                load(i, 0).start()
 
         @pl.when(s == -1)
         def _():
@@ -523,26 +550,28 @@
                 over_y(0, p).wait_recv()
                 over_x(0, p).start()
             wait_xr(0)
-            load(10, 0).start()
             load(3, 0).wait()
-            load(10, 0).wait()
-
-        for r in range(max(1, 16 // n)):
-            beat = s * 16 // n + r
-            on_beat = (s >= 0) & (lax.rem(s, max(1, n // 16)) == 0)
-            for t in range(1, len(tensors)):
-                p = beat + 2 - (first[t] - first[1])
-
-                @pl.when(on_beat & (p >= (2 if t == 1 else 0)) & (p < tensors[t][4]))
-                def _(t=t, p=p):
-                    over_y(t, p).start()
-
-                q = beat - 2 - (first[t] - first[1])
-
-                @pl.when(on_beat & (q >= 0) & (q < tensors[t][4]))
-                def _(t=t, q=q):
-                    over_y(t, q).wait_recv()
-                    over_x(t, q).start()
+
+        def pace(v):
+            return 2 + v * 5 // 6
+
+        new = (s == 0) | ((s > 0) & (pace(s) > pace(s - 1)))
+        late = s - 3
+        old = ((s > 0) & (s < 3)) | (late == 0) | ((late > 0) & (pace(late) > pace(late - 1)))
+        back = jnp.where(s < 3, s - 1, pace(late))
+        for t in range(1, len(tensors)):
+            p = pace(s) - (first[t] - first[1])
+
+            @pl.when(new & (p >= 0) & (p < tensors[t][4]))
+            def _(t=t, p=p):
+                over_y(t, p).start()
+
+            q = back - (first[t] - first[1])
+
+            @pl.when(old & (q >= 0) & (q < tensors[t][4]))
+            def _(t=t, q=q):
+                over_y(t, q).wait_recv()
+                over_x(t, q).start()
 
         for t, when, i in ((1, n // 2, 11), (2, 3 * n // 4, 12), (3, n - 1, 13)):
             @pl.when(s == when)
@@ -552,12 +581,13 @@
 
         @pl.when(s == n + n // 2)
         def _():
+            wait_sends(0)
             for t in (4, 5, 6, 7):
                 wait_xr(t)
             for i in (0, 1, 2, 3, 7, 8, 9, 10):
                 load(i, 1).start()
 
-        @pl.when(s == 2 * n)
+        @pl.when(s == 2 * n + 5)
         def _():
             for t in (8, 9, 10):
                 wait_xr(t)
@@ -568,7 +598,7 @@
 
     lax.fori_loop(0, 4 * n + FORWARD + AHEAD, lambda t, carry: slot(t - AHEAD, carry), 0)
 
-    for t in range(len(tensors)):
+    for t in range(1, len(tensors)):
         wait_sends(t)
     for na in (2 * n - 2, 2 * n - 1):
         kv_wait(na)
@@ -577,7 +607,38 @@
     halfs = h.at[0, pl.ds(0, S // 2)]
     rcopy(halfs, halfs, s_one.at[0], s_yh.at[0], ypart).wait_send()
     rcopy(halfs, halfs, s_one.at[1], s_one.at[2], sib).wait()
-    lcopy(x, h.at[y], s_one.at[3]).wait()
+
+
+def write_kernel(*refs):
+    k = len(refs) // 2
+    sems = refs[-1]
+    copies = []
+    for i in range(k):
+        src, dst = refs[i], refs[k + i]
+        for a in range(src.shape[0]):
+            for b in range(src.shape[1] if len(src.shape) > 3 else 4):
+                if len(src.shape) > 3:
+                    one, two = src.at[a, b], dst.at[a, b]
+                else:
+                    size = src.shape[1] // 4
+                    one, two = src.at[a, pl.ds(b * size, size)], dst.at[a, pl.ds(b * size, size)]
+                copies.append(pltpu.make_async_copy(one, two, sems.at[len(copies)]))
+    for copy in copies:
+        copy.start()
+    for copy in copies:
+        copy.wait()
+
+
+def write_out(*arrays):
+    return pl.pallas_call(
+        write_kernel,
+        out_shape=[jax.ShapeDtypeStruct(v.shape, v.dtype) for v in arrays],
+        in_specs=[pl.BlockSpec(memory_space=pltpu.VMEM)] * len(arrays),
+        out_specs=[pl.BlockSpec(memory_space=pl.ANY)] * len(arrays),
+        scratch_shapes=[pltpu.SemaphoreType.DMA((16,))],
+        compiler_params=pltpu.CompilerParams(vmem_limit_bytes=2**20),
+        name="write",
+    )(*arrays)
 
 
 def run_layers(hidden, lengths, w_query, w_key, w_value, w_out, w_gate, w_up, w_down, norm_attn, norm_mlp):
@@ -593,21 +654,23 @@
     outs = pl.pallas_call(
         functools.partial(layers_kernel, C),
         out_shape=[
-            jax.ShapeDtypeStruct((B, S, D), BF16),
-            jax.ShapeDtypeStruct((L, B, S, HD), BF16),
-            jax.ShapeDtypeStruct((L, B, S, HD), BF16),
+            pltpu.VMEM((B, S, D), BF16),
+            pltpu.VMEM((L, B, S, HD), BF16),
+            pltpu.VMEM((L, B, S, HD), BF16),
             jax.ShapeDtypeStruct((D, HD), BF16),
             jax.ShapeDtypeStruct((D, HD), BF16),
             jax.ShapeDtypeStruct((D, HD), BF16),
-            jax.ShapeDtypeStruct((L, HD, D), BF16),
+            jax.ShapeDtypeStruct((HD, D), BF16),
             jax.ShapeDtypeStruct((L, D, FL), BF16),
             jax.ShapeDtypeStruct((L, D, FL), BF16),
             jax.ShapeDtypeStruct((L, FL, D), BF16),
         ],
-        in_specs=[any_space, pl.BlockSpec(memory_space=pltpu.SMEM)] + [any_space] * 7 + [vmem, vmem, any_space],
-        out_specs=[any_space] * 10,
+        in_specs=[any_space] * 12,
+        out_specs=[vmem] * 3 + [any_space] * 7,
         scratch_shapes=[
-            pltpu.VMEM((S, D), BF16),
+            pltpu.SMEM((B,), jnp.int32),
+            pltpu.VMEM((L, D), F32),
+            pltpu.VMEM((L, D), F32),
             pltpu.VMEM((2, C, D), BF16),
             pltpu.VMEM((2, C, D), BF16),
             pltpu.VMEM((2, D, 3 * HD), BF16),
@@ -627,12 +690,13 @@
             pltpu.VMEM((RING, C // 2, D), BF16),
             pltpu.VMEM((RING, C // 2, D), BF16),
             pltpu.VMEM((RING, C // 4, D), BF16),
-            dma((14, RING)),
-            dma((RING,)),
-            dma((7,)),
+            dma((18, RING)),
+            dma((n,)),
+            dma((8,)),
             dma((2, 4)),
             dma((2, 4)),
-            dma((n,)),
+            dma((2,)),
+            dma((2,)),
             dma((2,)),
             dma((14,)),
             dma((11,)),
@@ -640,13 +704,13 @@
             dma((11,)),
             dma((32,)),
         ],
-        compiler_params=pltpu.CompilerParams(collective_id=0, has_side_effects=True, vmem_limit_bytes=66_000_000),
+        compiler_params=pltpu.CompilerParams(collective_id=0, has_side_effects=True, vmem_limit_bytes=43 * 2**20),
         name="layers",
     )(
         hidden, lengths, w_query.reshape(L, D, HD), w_key.reshape(L, D, HD), w_value.reshape(L, D, HD),
         w_out.reshape(L, HD, D), w_gate, w_up, w_down, norm_attn, norm_mlp, jnp.asarray(rope_table(S, HD)),
     )
-    h, kc, vc = outs[:3]
+    h, kc, vc = write_out(*outs[:3])
     return h, kc.reshape(L, B, 1, S, HD), vc.reshape(L, B, 1, S, HD)
 
 

time: 435 us -> 412 us (0.947)
  local copies, waits for them, and re-layouts: 18 us -> 0 us
  Pallas kernels: 416 us -> 411 us
    unnamed x7 -> x0, local copies, waits for them, and re-layouts: 18 us -> none
    pallas_call x1 -> x2, Pallas kernels: 416 us -> 411 us  [the longest x1 404 us: run_layers(): pl.pallas_call(functools.partial(layers_kernel, C), out_shape=[pltpu.VMEM...]
where the time goes in v3:
time: 412 us
  Pallas kernels  411 us (100%)
    pallas_call x1, Pallas kernels, run_layers(): pl.pallas_call(functools.partial(layers_kernel, C), out_shape=[pltpu.VMEM...  404 us

profile of v3, /device:TPU:0, one launch (start us, length us, event | category | flops | bytes accessed | tf_op | source)
XLA Modules:
  0.0 411.8 jit_solution(2158360958186631610)
XLA Ops:
  0.6 403.9 %layers.1 = (bf16[2,2048,2048]{2,1,0:T(8,128)(2,1)S(1)}, bf16[2,2,2048,128]{3,2,1,0:T(8,128)(2,1)S(1)}, bf16[2,2,2048,128]{3,2,1,0:T(8,128)(2,1)S(1)}, bf16[2048...) custom-call(bf16[2,2048,2048]{2,1,0:T(8,128)(2,1)} %hid.1, ...), custom_call_target="tpu_custom_call" | custom-call | tf_op jit(solution)/shard_map/layers/pallas_call | solution.py:654
  404.6 7.2 %write.1 = (bf16[2,2048,2048]{2,1,0:T(8,128)(2,1)}, bf16[2,2,2048,128]{3,2,1,0:T(8,128)(2,1)}, bf16[2,2,2048,128]{3,2,1,0:T(8,128)(2,1)}) custom-call(bf16[2,2048,2048]{2,1,0:T(8,128)(2,1)S(1)} %get-tuple-element.9.refs_0_, bf16[2,2,2048,128]{3,2,1,0:T(8,128)(2,1)S(1)} %get-tuple-element.10.refs_1_, bf16[2,2,2048,128]{3,2,1,0:T(8,128)(2,1)S(1)} %get-tuple-element.11.refs_2_), custom_call_target="tpu_custom_call" | custom-call | tf_op jit(solution)/shard_map/write/pallas_call | solution.py:633

commit v4 on v3

--- a/solution.py
+++ b/solution.py
@@ -12,10 +12,11 @@
 ROPE_BASE = 10000.0
 CHUNK = 128
 RING = 8
-EXCHANGE, FINISH, PASS, SHARE_B, SHARE_A, RETIRE, FORWARD = 1, 2, 4, 4, 5, 6, 7
+EXCHANGE, FINISH, PASS, SHARE_B, SHARE_A, RETIRE, FORWARD = 1, 2, 4, 3, 5, 6, 7
 (D2D_S, D2D_R, UP_S, UP_A0, UP_A1, UP_B, MID_S, MID_0, MID_1, FI_S, FI_0, FI_1,
  FO_S, FO_B, FO_A0, FO_A1, FS_S, FS_R) = range(18)
 AHEAD = 2
+ATTN_LOADS, MLP_LOADS = (0, 1, 2, 3, 7, 8, 9, 10), (4, 5, 6, 11, 12, 13)
 F32 = jnp.float32
 BF16 = jnp.bfloat16
 MESH = pl.DeviceIdType.MESH
@@ -32,7 +33,7 @@
 def layers_kernel(C, hid, lens_in, wq, wk, wv, wo, wg, wu, wd, ga_in, gm_in, rope,
                   h, kc, vc, lq, lk, lv, lo, lg, lu, ld,
                   lens, ga, gm, xo, a, wqkv, wov, wgv, wuv, wdv, ropev, kb, vb, sc, ob, osend, mb, pb, d2d, ts, ro, ri,
-                  s_ch, s_yh, s_one, s_kv, s_o, s_x, s_xo, s_rope, s_wl, s_ys, s_xs, s_xr, s_yr):
+                  s_ch, s_yh, s_one, s_kv, s_o, s_x, s_xo, s_rope, s_first, s_wl, s_ys, s_xs, s_xr, s_yr):
     _, S, D = hid.shape
     HD = wq.shape[2]
     FL = wg.shape[2]
@@ -70,14 +71,12 @@
     def _():
         pl.semaphore_signal(barrier, inc=1, device_id=outward, device_id_type=MESH)
 
-    pl.semaphore_wait(barrier, jnp.where(inner, 5, 4))
-
     def rcopy(src, dst, ss, rs, dev):
         return pltpu.make_async_remote_copy(src_ref=src, dst_ref=dst, send_sem=ss, recv_sem=rs, device_id=dev, device_id_type=MESH)
 
     lcopy = pltpu.make_async_copy
 
-    tensors = [(wo, 0, wov.at[pl.ds(HD, HD)], HD, 4), (wg, 0, lg.at[0], D, 4), (wu, 0, lu.at[0], D, 4), (wd, 0, ld.at[0], FL, 4),
+    tensors = [(wo, 0, wov.at[pl.ds(HD, HD)], HD, 1), (wg, 0, lg.at[0], D, 4), (wu, 0, lu.at[0], D, 4), (wd, 0, ld.at[0], FL, 4),
                (wq, 1, lq, D, 1), (wk, 1, lk, D, 1), (wv, 1, lv, D, 1), (wo, 1, lo, HD, 1),
                (wg, 1, lg.at[1], D, 4), (wu, 1, lu.at[1], D, 4), (wd, 1, ld.at[1], FL, 4)]
     first = [0]
@@ -109,6 +108,58 @@
     def wait_sends(t):
         rcopy(half_of(t), half_of(t), s_ys.at[t], s_yr.at[first[t]], ypart).wait_send()
         rcopy(half_of(t), half_of(t), s_xs.at[t], s_xr.at[t], xpart).wait_send()
+
+    N4 = D // 4
+
+    def block(b):
+        return pl.ds(b * N4, N4)
+
+    def first_y(b):
+        half = HD // 2
+        rows = pl.ds(pl.multiple_of(dp * half, half), half)
+        land = wov.at[pl.ds(pl.multiple_of(HD + dp * half, half), half), block(b)]
+        return rcopy(wo.at[0, rows, block(b)], land, s_ys.at[0], s_first.at[0, b], ypart)
+
+    def first_x(b):
+        half = HD // 2
+        land = wov.at[pl.ds(pl.multiple_of(HD + dp * half, half), half), block(b)]
+        return rcopy(land, land, s_xs.at[0], s_first.at[1, b], xpart)
+
+    def first_d2d(b):
+        return rcopy(pb.at[0, pl.ds(his, H2), block(b)], d2d.at[0, :, block(b)], s_ch.at[D2D_S, 0], s_first.at[2, b], sib)
+
+    def first_up(b):
+        first_d2d(b).wait_recv()
+
+        @pl.when(outer)
+        def _():
+            for off, recvs in ((off_a, (UP_A0, UP_A1)), (off_b, (UP_B, UP_B))):
+                for half in (0, 1):
+                    for r in range(half * H8, half * H8 + H8, RB):
+                        rr = pl.ds(pl.multiple_of(off + r, RB), RB)
+                        mine = pl.ds(pl.multiple_of(my + off + r, RB), RB)
+                        total = pb[0, mine, block(b)].astype(F32) + d2d[0, rr, block(b)].astype(F32)
+                        ts[0, rr, block(b)] = total.astype(BF16)
+                    rows = pl.ds(pl.multiple_of(off + half * H8, H8), H8)
+                    src, dst = ts.at[0, rows, block(b)], ro.at[0, rows, block(b)]
+                    rcopy(src, dst, s_ch.at[UP_S, 0], s_ch.at[recvs[half], 0], inward).start()
+
+    def first_chunk():
+        for b in range(4):
+            first_y(b).wait_recv()
+            first_x(b).start()
+        load(3, 0).wait()
+        o_copy(0).wait_recv()
+        o = jnp.concatenate([ob[0, 0], ob[0, 1]], axis=1)
+        for b in range(4):
+            first_x(b).wait_recv()
+            pb[0, :, block(b)] = jnp.dot(o, wov[:, block(b)], preferred_element_type=F32).astype(BF16)
+            first_d2d(b).start()
+            if b:
+                first_up(b - 1)
+        first_up(3)
+        out_proj(1)
+        h_d2d(1).start()
 
     def load(i, layer):
         j, kind = divmod(i, 7)
@@ -362,6 +413,11 @@
                 g = jnp.dot(a[0], wgv[j, :, f:f + FB], preferred_element_type=F32)
                 u = jnp.dot(a[0], wuv[j, :, f:f + FB], preferred_element_type=F32)
                 mb[:, j * FL + f:j * FL + f + FB] = (jax.nn.gelu(g, approximate=True) * u).astype(BF16)
+
+        @pl.when(s == n)
+        def _():
+            load(MLP_LOADS[-1], 0).wait()
+
         m = mb[...]
         for q in range(0, D, NBLK):
             pb[lax.rem(s, NB), :, q:q + NBLK] = jnp.dot(m, wdv[:, q:q + NBLK], preferred_element_type=F32).astype(BF16)
@@ -384,7 +440,10 @@
         return pb[kk, mine, :].astype(F32) + d2d[kk, rr, :].astype(F32) + ro[kk, rr, :].astype(F32)
 
     def exchange(k):
-        h_d2d(k).wait_recv()
+        @pl.when(k > 0)
+        def _():
+            h_d2d(k).wait_recv()
+
         kk = slot_of(k)
         for half in (0, 1):
             h_up(k, off_a, H8, UP_A0 + half).wait_recv()
@@ -468,9 +527,7 @@
             ok = ok & cond
         pl.when(ok)(lambda: what(k))
 
-    for p in range(tensors[0][4]):
-        over_y(0, p).start()
-    for i in (0, 1, 2):
+    for i in ATTN_LOADS[:4]:
         load(i, 0).start()
     x_load(0).start()
     xo_load(0).start()
@@ -482,35 +539,36 @@
         for r in range(0, S, KB):
             kb[j, r:r + KB, :] = jnp.zeros((KB, HD), BF16)
             vb[j, r:r + KB, :] = jnp.zeros((KB, HD), BF16)
-    for i in (0, 1, 2):
+    pl.semaphore_wait(barrier, jnp.where(inner, 5, 4))
+    for b in (0, 1):
+        first_y(b).start()
+    for i in ATTN_LOADS[:3]:
         load(i, 0).wait()
-    load(3, 0).start()
     for copy in small:
         copy.wait()
 
     def slot(s, carry):
         at(s - RETIRE, retire)
         at(s - SHARE_A, share_a, outer)
-        at(s - SHARE_B, share_b, outer)
         at(s - PASS, pass_on, inner)
         at(s - FORWARD, forward_out, s - FORWARD >= 3 * n)
 
         @pl.when(s == n)
         def _():
-            for i in (4, 5, 6, 11, 12, 13):
+            for i in MLP_LOADS[:-1]:
                 load(i, 0).wait()
 
         @pl.when(s == 3 * n)
         def _():
-            for i in (4, 5, 6, 11, 12, 13):
+            for i in MLP_LOADS:
                 load(i, 1).wait()
 
         @pl.when(s == 2 * n - AHEAD)
         def _():
-            for i in (0, 1, 2, 3, 7, 8, 9, 10):
+            for i in ATTN_LOADS:
                 load(i, 1).wait()
 
-        ok = (s >= 0) & (s < 4 * n)
+        ok = (s >= 2) & (s < 4 * n)
         is_mlp = lax.rem(s // n, 2) == 1
 
         @pl.when(ok & is_mlp)
@@ -521,36 +579,32 @@
         def _():
             out_proj(s)
 
-        at(s, lambda k: h_d2d(k).start())
-
-        at(s, send_up, outer & (s == 0))
-        u = s + AHEAD
-
-        @pl.when((u < n) | ((u >= 2 * n) & (u < 3 * n)))
-        def _():
-            attn(u)
-
+        at(s, lambda k: h_d2d(k).start(), s >= 2)
         at(s - EXCHANGE, exchange, inner)
         at(s - FINISH, finish, inner)
-        at(s, send_up, outer & (s > 0))
+        at(s - SHARE_B, share_b, outer)
+        at(s, send_up, outer & (s >= 1))
+        u = s + AHEAD
+
+        @pl.when((u < n) | ((u >= 2 * n) & (u < 3 * n)))
+        def _():
+            attn(u)
 
         @pl.when(s == -AHEAD)
         def _():
-            for p in range(2):
-                over_y(1, p).start()
+            for b in (2, 3):
+                first_y(b).start()
+
+        @pl.when(s == -1)
+        def _():
+            over_y(1, 0).start()
+            over_y(1, 1).start()
+            first_chunk()
 
         @pl.when(s == 2)
         def _():
-            for i in (4, 5, 6):
+            for i in MLP_LOADS[:3]:
                 load(i, 0).start()
-
-        @pl.when(s == -1)
-        def _():
-            for p in range(tensors[0][4]):
-                over_y(0, p).wait_recv()
-                over_x(0, p).start()
-            wait_xr(0)
-            load(3, 0).wait()
 
         def pace(v):
             return 2 + v * 5 // 6
@@ -584,14 +638,14 @@
             wait_sends(0)
             for t in (4, 5, 6, 7):
                 wait_xr(t)
-            for i in (0, 1, 2, 3, 7, 8, 9, 10):
+            for i in ATTN_LOADS:
                 load(i, 1).start()
 
         @pl.when(s == 2 * n + 5)
         def _():
             for t in (8, 9, 10):
                 wait_xr(t)
-            for i in (4, 5, 6, 11, 12, 13):
+            for i in MLP_LOADS:
                 load(i, 1).start()
 
         return carry
@@ -698,6 +752,7 @@
             dma((2,)),
             dma((2,)),
             dma((2,)),
+            dma((3, 4)),
             dma((14,)),
             dma((11,)),
             dma((11,)),

time: 412 us -> 410 us (level)
  no operation moved by 1% of the time
where the time goes in v4:
time: 410 us
  Pallas kernels  409 us (100%)
    pallas_call x1, Pallas kernels, run_layers(): pl.pallas_call(functools.partial(layers_kernel, C), out_shape=[pltpu.VMEM...  402 us

profile of v4, /device:TPU:0, one launch (start us, length us, event | category | flops | bytes accessed | tf_op | source)
XLA Modules:
  0.0 409.8 jit_solution(4815554602853885878)
XLA Ops:
  0.6 401.9 %layers.1 = (bf16[2,2048,2048]{2,1,0:T(8,128)(2,1)S(1)}, bf16[2,2,2048,128]{3,2,1,0:T(8,128)(2,1)S(1)}, bf16[2,2,2048,128]{3,2,1,0:T(8,128)(2,1)S(1)}, bf16[2048...) custom-call(bf16[2,2048,2048]{2,1,0:T(8,128)(2,1)} %hid.1, ...), custom_call_target="tpu_custom_call" | custom-call | tf_op jit(solution)/shard_map/layers/pallas_call | solution.py:708
  402.6 7.2 %write.1 = (bf16[2,2048,2048]{2,1,0:T(8,128)(2,1)}, bf16[2,2,2048,128]{3,2,1,0:T(8,128)(2,1)}, bf16[2,2,2048,128]{3,2,1,0:T(8,128)(2,1)}) custom-call(bf16[2,2048,2048]{2,1,0:T(8,128)(2,1)S(1)} %get-tuple-element.9.refs_0_, bf16[2,2,2048,128]{3,2,1,0:T(8,128)(2,1)S(1)} %get-tuple-element.10.refs_1_, bf16[2,2,2048,128]{3,2,1,0:T(8,128)(2,1)S(1)} %get-tuple-element.11.refs_2_), custom_call_target="tpu_custom_call" | custom-call | tf_op jit(solution)/shard_map/write/pallas_call | solution.py:687

commit v5 on v4

--- a/solution.py
+++ b/solution.py
@@ -548,25 +548,27 @@
         copy.wait()
 
     def slot(s, carry):
-        at(s - RETIRE, retire)
         at(s - SHARE_A, share_a, outer)
         at(s - PASS, pass_on, inner)
+        at(s - RETIRE, retire)
         at(s - FORWARD, forward_out, s - FORWARD >= 3 * n)
 
-        @pl.when(s == n)
-        def _():
-            for i in MLP_LOADS[:-1]:
-                load(i, 0).wait()
-
-        @pl.when(s == 3 * n)
-        def _():
-            for i in MLP_LOADS:
-                load(i, 1).wait()
-
-        @pl.when(s == 2 * n - AHEAD)
-        def _():
-            for i in ATTN_LOADS:
-                load(i, 1).wait()
+        @pl.when(s <= 3 * n)
+        def _():
+            @pl.when(s == n)
+            def _():
+                for i in MLP_LOADS[:-1]:
+                    load(i, 0).wait()
+
+            @pl.when(s == 3 * n)
+            def _():
+                for i in MLP_LOADS:
+                    load(i, 1).wait()
+
+            @pl.when(s == 2 * n - AHEAD)
+            def _():
+                for i in ATTN_LOADS:
+                    load(i, 1).wait()
 
         ok = (s >= 2) & (s < 4 * n)
         is_mlp = lax.rem(s // n, 2) == 1
@@ -580,73 +582,76 @@
             out_proj(s)
 
         at(s, lambda k: h_d2d(k).start(), s >= 2)
+        at(s, send_up, outer & (s == 1))
+        u = s + AHEAD
+
+        @pl.when((u < n) | ((u >= 2 * n) & (u < 3 * n)))
+        def _():
+            attn(u)
+
         at(s - EXCHANGE, exchange, inner)
         at(s - FINISH, finish, inner)
         at(s - SHARE_B, share_b, outer)
-        at(s, send_up, outer & (s >= 1))
-        u = s + AHEAD
-
-        @pl.when((u < n) | ((u >= 2 * n) & (u < 3 * n)))
-        def _():
-            attn(u)
-
-        @pl.when(s == -AHEAD)
-        def _():
-            for b in (2, 3):
-                first_y(b).start()
-
-        @pl.when(s == -1)
-        def _():
-            over_y(1, 0).start()
-            over_y(1, 1).start()
-            first_chunk()
-
-        @pl.when(s == 2)
-        def _():
-            for i in MLP_LOADS[:3]:
-                load(i, 0).start()
-
-        def pace(v):
-            return 2 + v * 5 // 6
-
-        new = (s == 0) | ((s > 0) & (pace(s) > pace(s - 1)))
-        late = s - 3
-        old = ((s > 0) & (s < 3)) | (late == 0) | ((late > 0) & (pace(late) > pace(late - 1)))
-        back = jnp.where(s < 3, s - 1, pace(late))
-        for t in range(1, len(tensors)):
-            p = pace(s) - (first[t] - first[1])
-
-            @pl.when(new & (p >= 0) & (p < tensors[t][4]))
-            def _(t=t, p=p):
-                over_y(t, p).start()
-
-            q = back - (first[t] - first[1])
-
-            @pl.when(old & (q >= 0) & (q < tensors[t][4]))
-            def _(t=t, q=q):
-                over_y(t, q).wait_recv()
-                over_x(t, q).start()
-
-        for t, when, i in ((1, n // 2, 11), (2, 3 * n // 4, 12), (3, n - 1, 13)):
-            @pl.when(s == when)
-            def _(t=t, i=i):
-                wait_xr(t)
-                load(i, 0).start()
-
-        @pl.when(s == n + n // 2)
-        def _():
-            wait_sends(0)
-            for t in (4, 5, 6, 7):
-                wait_xr(t)
-            for i in ATTN_LOADS:
-                load(i, 1).start()
-
-        @pl.when(s == 2 * n + 5)
-        def _():
-            for t in (8, 9, 10):
-                wait_xr(t)
-            for i in MLP_LOADS:
-                load(i, 1).start()
+        at(s, send_up, outer & (s > 1))
+        @pl.when(s < 2 * n + 6)
+        def _():
+            @pl.when(s == -AHEAD)
+            def _():
+                for b in (2, 3):
+                    first_y(b).start()
+
+            @pl.when(s == -1)
+            def _():
+                over_y(1, 0).start()
+                over_y(1, 1).start()
+                first_chunk()
+
+            @pl.when(s == 2)
+            def _():
+                for i in MLP_LOADS[:3]:
+                    load(i, 0).start()
+
+            def pace(v):
+                return 2 + v * 5 // 6
+
+            new = (s == 0) | ((s > 0) & (pace(s) > pace(s - 1)))
+            late = s - 3
+            old = ((s > 0) & (s < 3)) | (late == 0) | ((late > 0) & (pace(late) > pace(late - 1)))
+            back = jnp.where(s < 3, s - 1, pace(late))
+            for t in range(1, len(tensors)):
+                p = pace(s) - (first[t] - first[1])
+
+                @pl.when(new & (p >= 0) & (p < tensors[t][4]))
+                def _(t=t, p=p):
+                    over_y(t, p).start()
+
+                q = back - (first[t] - first[1])
+
+                @pl.when(old & (q >= 0) & (q < tensors[t][4]))
+                def _(t=t, q=q):
+                    over_y(t, q).wait_recv()
+                    over_x(t, q).start()
+
+            for t, when, i in ((1, n // 2, 11), (2, 3 * n // 4, 12), (3, n - 1, 13)):
+                @pl.when(s == when)
+                def _(t=t, i=i):
+                    wait_xr(t)
+                    load(i, 0).start()
+
+            @pl.when(s == n + n // 2)
+            def _():
+                wait_sends(0)
+                for t in (4, 5, 6, 7):
+                    wait_xr(t)
+                for i in ATTN_LOADS:
+                    load(i, 1).start()
+
+            @pl.when(s == 2 * n + 5)
+            def _():
+                for t in (8, 9, 10):
+                    wait_xr(t)
+                for i in MLP_LOADS:
+                    load(i, 1).start()
 
         return carry
 

time: 410 us -> 409 us (level)
  no operation moved by 1% of the time
where the time goes in v5:
time: 409 us
  Pallas kernels  408 us (100%)
    pallas_call x1, Pallas kernels, run_layers(): pl.pallas_call(functools.partial(layers_kernel, C), out_shape=[pltpu.VMEM...  401 us

profile of v5, /device:TPU:0, one launch (start us, length us, event | category | flops | bytes accessed | tf_op | source)
XLA Modules:
  0.0 408.8 jit_solution(6845466112504945746)
XLA Ops:
  0.6 401.0 %layers.1 = (bf16[2,2048,2048]{2,1,0:T(8,128)(2,1)S(1)}, bf16[2,2,2048,128]{3,2,1,0:T(8,128)(2,1)S(1)}, bf16[2,2,2048,128]{3,2,1,0:T(8,128)(2,1)S(1)}, bf16[2048...) custom-call(bf16[2,2048,2048]{2,1,0:T(8,128)(2,1)} %hid.1, ...), custom_call_target="tpu_custom_call" | custom-call | tf_op jit(solution)/shard_map/layers/pallas_call | solution.py:713
  401.6 7.2 %write.1 = (bf16[2,2048,2048]{2,1,0:T(8,128)(2,1)}, bf16[2,2,2048,128]{3,2,1,0:T(8,128)(2,1)}, bf16[2,2,2048,128]{3,2,1,0:T(8,128)(2,1)}) custom-call(bf16[2,2048,2048]{2,1,0:T(8,128)(2,1)S(1)} %get-tuple-element.9.refs_0_, bf16[2,2,2048,128]{3,2,1,0:T(8,128)(2,1)S(1)} %get-tuple-element.10.refs_1_, bf16[2,2,2048,128]{3,2,1,0:T(8,128)(2,1)S(1)} %get-tuple-element.11.refs_2_), custom_call_target="tpu_custom_call" | custom-call | tf_op jit(solution)/shard_map/write/pallas_call | solution.py:692

commit v6 on v5

--- a/solution.py
+++ b/solution.py
@@ -431,7 +431,9 @@
                     rr = pl.ds(pl.multiple_of(off + r, RB), RB)
                     mine = pl.ds(pl.multiple_of(my + off + r, RB), RB)
                     ts[kk, rr, :] = (pb[kk, mine, :].astype(F32) + d2d[kk, rr, :].astype(F32)).astype(BF16)
-                h_up(k, off + half * H8, H8, recvs[half]).start()
+                if off is off_a:
+                    h_up(k, off + half * H8, H8, recvs[half]).start()
+        h_up(k, off_b, H4, UP_B).start()
 
     def part(k, off, r):
         kk = slot_of(k)
@@ -464,7 +466,7 @@
                 total = part(k, off_b, r) + ri[kk, r:r + RB, :].astype(F32)
                 x[rows, :] = (x[rows, :].astype(F32) + total).astype(BF16)
             h_fi(k, off_b + half * H8, FI_0 + half, H8).start()
-            h_fo(k, off_b + half * H8, FO_B, H8, outward).start()
+        h_fo(k, off_b, FO_B, H4, outward).start()
         h_fs(k, off_b, H4).start()
 
         @pl.when(last_stage(k))
@@ -476,11 +478,12 @@
             off = off_a + half * H8
             h_fi(k, off, FI_0 + half, H8).wait_recv()
             h_fo(k, off, FO_A0 + half, H8, outward).start()
-            h_fs(k, off, H8).start()
 
             @pl.when(last_stage(k))
             def _(off=off):
                 h_yh(k, off, H8).start()
+
+        h_fs(k, off_a, H4).start()
 
     def share_b(k):
         h_fo(k, off_b, FO_B, H4, inward).wait_recv()
@@ -494,11 +497,12 @@
         for half in (0, 1):
             off = off_a + half * H8
             h_fo(k, off, FO_A0 + half, H8, inward).wait_recv()
-            h_fs(k, off, H8).start()
 
             @pl.when(last_stage(k))
             def _(off=off):
                 h_yh(k, off, H8).start()
+
+        h_fs(k, off_a, H4).start()
 
     def retire(k):
         h_fs(k, 0, H2).wait_recv()

time: 409 us -> 409 us (level)
  no operation moved by 1% of the time
where the time goes in v6:
time: 409 us
  Pallas kernels  408 us (100%)
    pallas_call x1, Pallas kernels, run_layers(): pl.pallas_call(functools.partial(layers_kernel, C), out_shape=[pltpu.VMEM...  401 us

profile of v6, /device:TPU:0, one launch (start us, length us, event | category | flops | bytes accessed | tf_op | source)
XLA Modules:
  0.0 408.6 jit_solution(15196784267266288554)
XLA Ops:
  0.6 400.8 %layers.1 = (bf16[2,2048,2048]{2,1,0:T(8,128)(2,1)S(1)}, bf16[2,2,2048,128]{3,2,1,0:T(8,128)(2,1)S(1)}, bf16[2,2,2048,128]{3,2,1,0:T(8,128)(2,1)S(1)}, bf16[2048...) custom-call(bf16[2,2048,2048]{2,1,0:T(8,128)(2,1)} %hid.1, ...), custom_call_target="tpu_custom_call" | custom-call | tf_op jit(solution)/shard_map/layers/pallas_call | solution.py:717
  401.4 7.2 %write.1 = (bf16[2,2048,2048]{2,1,0:T(8,128)(2,1)}, bf16[2,2,2048,128]{3,2,1,0:T(8,128)(2,1)}, bf16[2,2,2048,128]{3,2,1,0:T(8,128)(2,1)}) custom-call(bf16[2,2048,2048]{2,1,0:T(8,128)(2,1)S(1)} %get-tuple-element.9.refs_0_, bf16[2,2,2048,128]{3,2,1,0:T(8,128)(2,1)S(1)} %get-tuple-element.10.refs_1_, bf16[2,2,2048,128]{3,2,1,0:T(8,128)(2,1)S(1)} %get-tuple-element.11.refs_2_), custom_call_target="tpu_custom_call" | custom-call | tf_op jit(solution)/shard_map/write/pallas_call | solution.py:696
